TPU v7x, 256 devices: a whole 4x4x8 slice. The times are simulated.
256 devices in a mesh: rep: 4 (over y), row: 4 (over z_hi), col: 16 (over z_lo, x, core).
Axes of the slice: x: 4, y: 4, z: 8 (z_hi: 4, z_lo: 2; z = z_hi * 2 + z_lo), core: 2. Of those that a mesh axis runs over, the one named last changes fastest.
Arguments:
- patches: bfloat16 [4096, 588], P(('rep', 'col')), may hold values from -20 to 20
- embed_weight: bfloat16 [588, 6144], P(None, 'row'), may hold values from -1 to 1
- embed_bias: float32 [6144], P('row'), may hold values from -3 to 3
- old_in: bfloat16 [64, 768, 1536], P(('row', 'col')), may hold values from -0.078125 to 0.078125
- old_out: bfloat16 [64, 1536, 768], P(('row', 'col')), may hold values from -0.0546875 to 0.0546875
- restore_id: int32 [1], replicated, may hold values from 0 to 47
- norm_gains: float32 [48, 6144], P(None, 'row'), may hold values from 0.1 to 1.9
- in_biases: float32 [48, 12288], P(None, 'col'), may hold values from -3 to 3
- out_biases: float32 [48, 6144], P(None, 'row'), may hold values from -3 to 3
- final_gain: float32 [6144], P('row'), may hold values from 0.1 to 1.9
- check_weight: bfloat16 [6144, 128], P('row'), may hold values from -0.078125 to 0.078125
Outputs:
- in_weight: bfloat16 [6144, 12288], P('row', 'col')
- out_weight: bfloat16 [12288, 6144], P('col', 'row')
- check_logits: float32 [4096, 128], P(('rep', 'col'))
All inputs are finite; a program needn't handle non-finite values.
Results may differ from a plain program's by a relative error of at most 0.0062.
Values may be sent and summed in bfloat16 or wider, within the bound.
A program may use at most 64 MiB of HBM per device.

v0:
```python
import jax
import jax.numpy as jnp
from jax import lax
from jax.sharding import PartitionSpec as P

EPSILON = 1e-06


def from_everyone(shard, axis):
    size = lax.axis_size(axis)
    return lax.all_to_all(
        jnp.broadcast_to(shard[None], (size, *shard.shape)), axis, 0, 0, tiled=True
    )


def taken_together(shard, axis):
    return from_everyone(shard, axis).sum(axis=0)


def packed_total(arrays, axis):
    ends = [0]
    for a in arrays:
        ends.append(ends[-1] + a.size)
    so_far = taken_together(jnp.concatenate([a.ravel() for a in arrays]), axis)
    return tuple((so_far[b:e].reshape(a.shape) for a, b, e in zip(arrays, ends, ends[1:])))


def for_sending(shard):
    return jax.tree.map(lambda a: a.astype(jnp.bfloat16) if a.dtype == jnp.float32 else a, shard)


def partner(value, axis, bit):
    mask = 2**bit
    pairs = [(source, source ^ mask) for source in range(lax.axis_size(axis))]
    return lax.ppermute(value, axis, pairs)


def rows_first(arrays, axis, dims):
    turned = [jnp.moveaxis(a, dim, 0) for a, dim in zip(arrays, dims)]
    widths = [t[0].size for t in turned]
    both = jnp.concatenate([t.reshape(-1, w) for t, w in zip(turned, widths)], axis=1)
    out = lax.all_gather(both, axis, axis=0, tiled=True)
    parts = jnp.split(out, [sum(widths[:k]) for k in range(1, len(widths))], axis=1)
    return tuple(
        (
            jnp.moveaxis(b.reshape(-1, *t.shape[1:]), 0, dim)
            for b, t, dim in zip(parts, turned, dims)
        )
    )


def cut_along(shard, dim, size):
    before, after = (shard.shape[:dim], shard.shape[dim + 1 :])
    return jnp.moveaxis(shard.reshape(*before, size, -1, *after), dim, 0)


def sent_and_summed(shard, axis, dim):
    size = lax.axis_size(axis)
    parts = lax.all_to_all(cut_along(shard, dim, size), axis, 0, 0, tiled=True)
    return jnp.sum(parts.astype(jnp.float32), axis=0)


def laid_out(parts, dim):
    shape = list(parts.shape[1:])
    shape[dim] *= parts.shape[0]
    return jnp.moveaxis(parts, 0, dim).reshape(shape)


def gathered_copies(shard, axis, dim):
    parts = from_everyone(shard, axis)
    return laid_out(parts, dim)


def pick_rows(restore_id, param_table):
    selector = (
        jnp.arange(param_table.shape[0], dtype=jnp.int32)[None, :] == restore_id[:, None]
    ).astype(jnp.float32)
    return jnp.dot(selector, param_table, precision=lax.Precision.HIGHEST)[0]


def norm_rows(values, gain_row):
    feature_count = values.shape[1] * lax.axis_size("row")
    totals = packed_total((jnp.sum(values, axis=1), jnp.sum(values * values, axis=1)), "row")
    average = totals[0][:, None] / feature_count
    spread = totals[1][:, None] / feature_count - average * average
    return ((values - average) * lax.rsqrt(spread + EPSILON) * gain_row).astype(jnp.bfloat16)


def move_halves(pieces, bit_total, device_index, exchange):
    for bit_number in range(bit_total):
        upper_side = device_index >> bit_number & 1 == 1
        outgoing = tuple(
            (jnp.where(upper_side, lower_part, upper_part) for lower_part, upper_part in pieces)
        )
        incoming = exchange(outgoing, bit_number)
        pieces = tuple(
            (
                (
                    jnp.where(upper_side, arrived, lower_part),
                    jnp.where(upper_side, upper_part, arrived),
                )
                for (lower_part, upper_part), arrived in zip(pieces, incoming)
            )
        )
    return pieces


def on_device(
    patches,
    embed_weight,
    embed_bias,
    old_in,
    old_out,
    restore_id,
    norm_gains,
    in_biases,
    out_biases,
    final_gain,
    check_weight,
):
    tiles_here, tile_rows, tile_cols = old_in.shape
    local_cols = tiles_here * tile_cols
    half_cols = local_cols // 2
    in_local = jnp.transpose(old_in, (1, 0, 2)).reshape(tile_rows, local_cols)
    out_local = old_out.reshape(local_cols, tile_rows)
    col_index = lax.axis_index("col")
    col_count = lax.axis_size("col")
    col_bits = col_count.bit_length() - 1
    share_rows = tile_rows // lax.axis_size("rep")
    first_row = lax.axis_index("rep") * share_rows
    in_share = lax.dynamic_slice_in_dim(in_local, first_row, share_rows, 0)
    out_share = lax.dynamic_slice_in_dim(out_local, first_row, share_rows, 1)
    pieces = (
        (in_share[:, :half_cols], in_share[:, half_cols:]),
        (out_share[:half_cols], out_share[half_cols:]),
    )
    pieces = move_halves(
        pieces,
        col_bits,
        col_index,
        lambda send_parts, bit_number: jax.tree.map(
            lambda part, own: part.astype(own.dtype),
            partner(for_sending(send_parts), "col", bit_number),
            send_parts,
        ),
    )
    gathered = rows_first(
        (pieces[0][0], pieces[0][1], pieces[1][0], pieces[1][1]), "rep", (0, 0, 1, 1)
    )
    in_weight = jnp.concatenate((gathered[0], gathered[1]), axis=0)
    out_weight = jnp.concatenate((gathered[2], gathered[3]), axis=1)
    layer_gain = pick_rows(restore_id, norm_gains)
    in_bias = pick_rows(restore_id, in_biases)
    out_bias = pick_rows(restore_id, out_biases)
    embedded = jnp.dot(patches, embed_weight, preferred_element_type=jnp.float32) + embed_bias
    normed = norm_rows(embedded, layer_gain)
    partial_pre = jnp.dot(
        lax.all_gather(normed, "col", axis=0, tiled=True),
        in_weight,
        preferred_element_type=jnp.float32,
    )
    pre_share = sent_and_summed(partial_pre.astype(jnp.bfloat16), "row", 0) + in_bias
    hidden = jax.nn.gelu(pre_share, approximate=False).astype(jnp.bfloat16)
    partial_branch = jnp.dot(
        gathered_copies(hidden, "row", 0), out_weight, preferred_element_type=jnp.float32
    )
    updated = embedded + sent_and_summed(partial_branch.astype(jnp.bfloat16), "col", 0) + out_bias
    final_normed = norm_rows(updated, final_gain)
    check_logits = lax.psum(
        jnp.dot(final_normed, check_weight, preferred_element_type=jnp.float32), "row"
    )
    return (in_weight, out_weight, check_logits)


def solution(mesh):
    placed = (
        P(("rep", "col"), None),
        P(None, "row"),
        P("row"),
        P(("row", "col"), None, None),
        P(("row", "col"), None, None),
        P(),
        P(None, "row"),
        P(None, "col"),
        P(None, "row"),
        P("row"),
        P("row", None),
    )
    return jax.shard_map(
        on_device,
        mesh=mesh,
        in_specs=placed,
        out_specs=(P("row", "col"), P("col", "row"), P(("rep", "col"), None)),
        check_vma=False,
    )
```

profile of v0, /device:TPU:24, one launch (start us, length us, event | category | flops | bytes accessed | tf_op | source)
XLA Modules:
  0.0 345.1 jit_solution(2980738248300091822)
XLA Ops:
  7.2 1.6 copy-done
  9.6 2.4 constant_dynamic-slice_fusion
  12.0 1.1 copy.25
  13.2 1.2 copy.26
  15.6 1.7 broadcast_select_fusion.12
  17.3 1.5 collective-permute-start.1
  18.8 1.7 broadcast_select_fusion.2
  21.0 6.4 %collective-permute-done.1 = bf16[192,768]{1,0:T(8,128)(2,1)} collective-permute-done((bf16[192,768]{1,0:T(8,128)(2,1)}, bf16[192,768]{1,0:T(8,128)(2,1)}, u32[]{:S(2)}, u32[]{:S(2)}) %collective-permute-start.1) | collective-permute-done | bytes 294944 | tf_op jit(solution)/shard_map/ppermute | solution.py:35
  27.5 2.0 broadcast_select_fusion.15
  29.5 3.0 collective-permute-start.2
  32.6 0.9 collective-permute-done.5
  33.5 2.0 broadcast_select_fusion.5
  35.5 3.4 collective-permute-start.6
  38.9 3.5 %collective-permute-done.2 = bf16[192,768]{1,0:T(8,128)(2,1)} collective-permute-done((bf16[192,768]{1,0:T(8,128)(2,1)}, bf16[192,768]{1,0:T(8,128)(2,1)}, u32[]{:S(2)}, u32[]{:S(2)}) %collective-permute-start.2) | collective-permute-done | bytes 294944 | tf_op jit(solution)/shard_map/ppermute | solution.py:35
  42.3 1.1 broadcast_select_fusion.18
  43.4 2.0 collective-permute-start.3
  45.4 2.2 collective-permute-done.6
  47.7 1.1 broadcast_select_fusion.6
  48.8 2.0 collective-permute-start.7
  50.8 1.0 broadcast_select_fusion.17
  51.8 5.3 %collective-permute-done.7 = bf16[768,192]{0,1:T(8,128)(2,1)S(1)} collective-permute-done((bf16[768,192]{0,1:T(8,128)(2,1)S(1)}, bf16[768,192]{0,1:T(8,128)(2,1)S(1)}, u32[]{:S(2)}, u32[]{:S(2)}) %collective-permute-start.7) | collective-permute-done | bytes 294944 | tf_op jit(solution)/shard_map/ppermute | solution.py:35
  57.1 1.0 select_bitcast_fusion.1
  58.1 1.2 pad_maximum_fusion.2
  59.3 2.1 fusion.21
  62.2 8.3 %all-to-all-start = ((f32[4,1,128]{2,1,0:T(1,128)}), f32[4,1,128]{2,1,0:T(1,128)S(1)}, u32[]{:S(2)}, u32[]{:S(2)}) async-start(f32[4,1,128]{2,1,0:T(1,128)} %broadcast_in_dim.6), calls=%async_computation | async-start | bytes 4096 | tf_op jit(solution)/shard_map/all_to_all | solution.py:11
  71.3 6.7 %all-to-all-done = f32[4,1,128]{2,1,0:T(1,128)S(1)} async-done(((f32[4,1,128]{2,1,0:T(1,128)}), f32[4,1,128]{2,1,0:T(1,128)S(1)}, u32[]{:S(2)}, u32[]{:S(2)}) %all-to-all-start) | async-done | bytes 2080 | tf_op jit(solution)/shard_map/all_to_all | solution.py:11
  78.2 0.8 multiply_convert_fusion.1
  79.0 34.0 %all-gather.3.cloned.1.call-done = bf16[768,3072]{1,0:T(8,128)(2,1)} async-done(((bf16[192,3072]{1,0:T(8,128)(2,1)}), bf16[768,3072]{1,0:T(8,128)(2,1)}) %all-gather.3.cloned.1.call-update) | async-done | bytes 4718608 | tf_op jit(solution)/shard_map/all_gather | solution.py:42
  113.0 3.8 %slice_bitcast_fusion.1 = (bf16[768,768]{0,1:T(8,128)(2,1)S(1)}, bf16[768,768]{0,1:T(8,128)(2,1)}, bf16[768,768]{1,0:T(8,128)(2,1)S(1)}, bf16[768,768]{1,0:T(8,128)(2,1)S(1)}) fusion(bf16[768,3072]{1,0:T(8,128)(2,1)} %all-gather.3.cloned.1.call-done), kind=kLoop, calls=%fused_computation.9 | loop fusion | bytes 9437184 | tf_op jit(solution)/shard_map/transpose | solution.py:46
  116.8 1.6 pad_maximum_fusion
  118.3 36.5 %all-gather.5.cloned.1.call-done = bf16[1024,1536]{1,0:T(8,128)(2,1)} async-done(((bf16[64,1536]{1,0:T(8,128)(2,1)}), bf16[1024,1536]{1,0:T(8,128)(2,1)}) %all-gather.5.cloned.1.call-update) | async-done | bytes 3145744 | tf_op jit(solution)/shard_map/all_gather | solution.py:158
  154.8 6.4 %convolution_convert_fusion.1 = bf16[1024,768]{1,0:T(8,128)(2,1)} fusion(bf16[1024,1536]{1,0:T(8,128)(2,1)} %all-gather.5.cloned.1.call-done, bf16[1536,768]{1,0:T(8,128)(2,1)} %pad_maximum_fusion), kind=kOutput, calls=%fused_computation.6 | convolution fusion | flops 2416705536 | bytes 7077888 | tf_op jit(solution)/shard_map/dot_general | solution.py:157
  161.2 6.8 %all-to-all-start.1 = ((bf16[4,256,768]{2,1,0:T(8,128)(2,1)}), bf16[4,256,768]{2,1,0:T(8,128)(2,1)}, u32[]{:S(2)}, u32[]{:S(2)}) async-start(bf16[4,256,768]{2,1,0:T(8,128)(2,1)} %bitcast.54), calls=%async_computation.1 | async-start | bytes 3145728 | tf_op jit(solution)/shard_map/all_to_all | solution.py:59
  168.0 1.1 convolution_reduce_fusion.2
  169.1 39.0 %all-to-all-done.1 = bf16[4,256,768]{2,1,0:T(8,128)(2,1)} async-done(((bf16[4,256,768]{2,1,0:T(8,128)(2,1)}), bf16[4,256,768]{2,1,0:T(8,128)(2,1)}, u32[]{:S(2)}, u32[]{:S(2)}) %all-to-all-start.1) | async-done | bytes 1572896 | tf_op jit(solution)/shard_map/all_to_all | solution.py:59
  208.1 1.7 convert_reduce_fusion.1
  209.8 1.7 fusion.2
  211.6 37.8 %all_to_all.27 = bf16[4,256,768]{2,1,0:T(8,128)(2,1)S(1)} all-to-all(bf16[4,256,768]{2,1,0:T(8,128)(2,1)S(1)} %broadcast_in_dim.7), channel_id=1, replica_groups=mesh['rep'=4,'row'=4,'col'=16] {'row'}, dimensions={0} | all-to-all | bytes 3145728 | tf_op jit(solution)/shard_map/all_to_all | solution.py:11
  249.4 4.9 %convolution_convert_fusion = bf16[1024,1536]{1,0:T(8,128)(2,1)} fusion(bf16[1024,768]{1,0:T(8,128)(2,1)S(1)} %bitcast.55, bf16[768,768]{0,1:T(8,128)(2,1)S(1)} %copy-done.1, bf16[768,768]{0,1:T(8,128)(2,1)S(1)} %get-tuple-element.26), kind=kOutput, calls=%fused_computation.1 | convolution fusion | flops 2422210560 | bytes 7077888 | tf_op jit(solution)/shard_map/dot_general | solution.py:164
  254.3 7.1 %all-to-all-start.3 = ((bf16[16,64,1536]{2,1,0:T(8,128)(2,1)}), bf16[16,64,1536]{2,1,0:T(8,128)(2,1)}, u32[]{:S(2)}, u32[]{:S(2)}) async-start(bf16[16,64,1536]{2,1,0:T(8,128)(2,1)} %bitcast.53), calls=%async_computation.3 | async-start | bytes 6291456 | tf_op jit(solution)/shard_map/all_to_all | solution.py:59
  261.4 1.2 convolution_reduce_fusion
  262.6 40.0 %all-to-all-done.3 = bf16[16,64,1536]{2,1,0:T(8,128)(2,1)} async-done(((bf16[16,64,1536]{2,1,0:T(8,128)(2,1)}), bf16[16,64,1536]{2,1,0:T(8,128)(2,1)}, u32[]{:S(2)}, u32[]{:S(2)}) %all-to-all-start.3) | async-done | bytes 3145760 | tf_op jit(solution)/shard_map/all_to_all | solution.py:59
  302.6 2.4 convert_reduce_fusion
  305.1 0.9 fusion.20
  306.7 3.2 all-to-all-start.4
  309.9 2.8 pad_maximum_fusion.1
  312.7 4.3 %copy.23 = bf16[768,1536]{1,0:T(8,128)(2,1)} copy(bf16[768,1536]{0,1:T(8,128)(2,1)} %pad_maximum_fusion.1) | data formatting | bytes 4718592
  317.9 20.4 %psum.7 = f32[64,128]{1,0:T(8,128)} all-reduce(f32[64,128]{1,0:T(8,128)S(1)} %fusion.10), channel_id=1, replica_groups=mesh['rep'=4,'row'=4,'col'=16] {'row'}, use_global_device_ids=true, to_apply=%region_8.9 | all-reduce | flops 8192 | bytes 65536 | tf_op jit(solution)/shard_map/psum | solution.py:169
  (50 shorter events, 5.3 us)
Async XLA Ops:
  7.2 1.7 copy-start
  7.2 105.8 %all-gather.3.cloned.1.call-start = ((), (), s32[]{:S(2)}) async-start(), calls=%async_computation.5 | async-start | bytes 5898240 | tf_op jit(solution)/shard_map/all_gather | solution.py:42
  9.6 5.9 %collective-permute-start = (bf16[192,768]{1,0:T(8,128)(2,1)}, bf16[192,768]{1,0:T(8,128)(2,1)}, u32[]{:S(2)}, u32[]{:S(2)}) collective-permute-start(bf16[192,768]{1,0:T(8,128)(2,1)} %broadcast_select_fusion.9), channel_id=1, source_target_pairs={{0,1},{1,0},{2,3},{3,2},{4,5},{5,4},{6,7},{7,6},{8,9},{9,8},{10,11... | collective-permute-start | bytes 884744 | tf_op jit(solution)/shard_map/ppermute | solution.py:35
  15.1 3.7 %collective-permute-start.4 = (bf16[768,192]{0,1:T(8,128)(2,1)}, bf16[768,192]{0,1:T(8,128)(2,1)}, u32[]{:S(2)}, u32[]{:S(2)}) collective-permute-start(bf16[768,192]{0,1:T(8,128)(2,1)} %bitcast_select_fusion.1), channel_id=1, source_target_pairs={{0,1},{1,0},{2,3},{3,2},{4,5},{5,4},{6,7},{7,6},{8,9},{9,8},{10,11... | collective-permute-start | bytes 884744 | tf_op jit(solution)/shard_map/ppermute | solution.py:35
  17.3 10.2 %collective-permute-start.1 = (bf16[192,768]{1,0:T(8,128)(2,1)}, bf16[192,768]{1,0:T(8,128)(2,1)}, u32[]{:S(2)}, u32[]{:S(2)}) collective-permute-start(bf16[192,768]{1,0:T(8,128)(2,1)} %broadcast_select_fusion.12), channel_id=1, source_target_pairs={{0,2},{1,3},{2,0},{3,1},{4,6},{5,7},{6,4},{7,5},{8,10},{9,11},{10,... | collective-permute-start | bytes 884744 | tf_op jit(solution)/shard_map/ppermute | solution.py:35
  20.5 13.0 %collective-permute-start.5 = (bf16[768,192]{0,1:T(8,128)(2,1)}, bf16[768,192]{0,1:T(8,128)(2,1)}, u32[]{:S(2)}, u32[]{:S(2)}) collective-permute-start(bf16[768,192]{0,1:T(8,128)(2,1)} %broadcast_select_fusion.2), channel_id=1, source_target_pairs={{0,2},{1,3},{2,0},{3,1},{4,6},{5,7},{6,4},{7,5},{8,10},{9,11},{10,... | collective-permute-start | bytes 884744 | tf_op jit(solution)/shard_map/ppermute | solution.py:35
  29.5 21.3 %copy-start.4 = (bf16[192,768]{1,0:T(8,128)(2,1)S(1)}, bf16[192,768]{1,0:T(8,128)(2,1)}, u32[]{:S(2)}) copy-start(bf16[192,768]{1,0:T(8,128)(2,1)} %get-tuple-element.21) | copy-start | bytes 884740
  29.5 21.3 %copy-start.5 = (bf16[192,768]{1,0:T(8,128)(2,1)S(1)}, bf16[192,768]{1,0:T(8,128)(2,1)}, u32[]{:S(2)}) copy-start(bf16[192,768]{1,0:T(8,128)(2,1)} %get-tuple-element.22) | copy-start | bytes 884740
  29.5 12.8 %collective-permute-start.2 = (bf16[192,768]{1,0:T(8,128)(2,1)}, bf16[192,768]{1,0:T(8,128)(2,1)}, u32[]{:S(2)}, u32[]{:S(2)}) collective-permute-start(bf16[192,768]{1,0:T(8,128)(2,1)} %get-tuple-element.20), channel_id=1, source_target_pairs={{0,4},{1,5},{2,6},{3,7},{4,0},{5,1},{6,2},{7,3},{8,12},{9,13},{10,... | collective-permute-start | bytes 884744 | tf_op jit(solution)/shard_map/ppermute | solution.py:35
  35.5 21.6 %copy-start.6 = (bf16[768,192]{0,1:T(8,128)(2,1)S(1)}, bf16[768,192]{0,1:T(8,128)(2,1)}, u32[]{:S(2)}) copy-start(bf16[768,192]{0,1:T(8,128)(2,1)} %get-tuple-element.24) | copy-start | bytes 884740
  35.5 21.6 %copy-start.7 = (bf16[768,192]{0,1:T(8,128)(2,1)S(1)}, bf16[768,192]{0,1:T(8,128)(2,1)}, u32[]{:S(2)}) copy-start(bf16[768,192]{0,1:T(8,128)(2,1)} %get-tuple-element.25) | copy-start | bytes 884740
  35.5 12.2 %collective-permute-start.6 = (bf16[768,192]{0,1:T(8,128)(2,1)}, bf16[768,192]{0,1:T(8,128)(2,1)}, u32[]{:S(2)}, u32[]{:S(2)}) collective-permute-start(bf16[768,192]{0,1:T(8,128)(2,1)} %get-tuple-element.23), channel_id=1, source_target_pairs={{0,4},{1,5},{2,6},{3,7},{4,0},{5,1},{6,2},{7,3},{8,12},{9,13},{10,... | collective-permute-start | bytes 884744 | tf_op jit(solution)/shard_map/ppermute | solution.py:35
  43.4 7.4 %collective-permute-start.3 = (bf16[192,768]{1,0:T(8,128)(2,1)S(1)}, bf16[192,768]{1,0:T(8,128)(2,1)S(1)}, u32[]{:S(2)}, u32[]{:S(2)}) collective-permute-start(bf16[192,768]{1,0:T(8,128)(2,1)S(1)} %broadcast_select_fusion.18), channel_id=1, source_target_pairs={{0,8},{1,9},{2,10},{3,11},{4,12},{5,13},{6,14},{7,15},{8,0},{9,1},... | collective-permute-start | bytes 884744 | tf_op jit(solution)/shard_map/ppermute | solution.py:35
  48.8 8.3 %collective-permute-start.7 = (bf16[768,192]{0,1:T(8,128)(2,1)S(1)}, bf16[768,192]{0,1:T(8,128)(2,1)S(1)}, u32[]{:S(2)}, u32[]{:S(2)}) collective-permute-start(bf16[768,192]{0,1:T(8,128)(2,1)S(1)} %broadcast_select_fusion.6), channel_id=1, source_target_pairs={{0,8},{1,9},{2,10},{3,11},{4,12},{5,13},{6,14},{7,15},{8,0},{9,1},... | collective-permute-start | bytes 884744 | tf_op jit(solution)/shard_map/ppermute | solution.py:35
  51.8 7.5 %copy-start.11 = (f32[1536]{0:T(1024)S(1)}, f32[1536]{0:T(1024)}, u32[]{:S(2)}) copy-start(f32[1536]{0:T(1024)} %param.13) | copy-start | bytes 18436
  58.1 13.0 %copy-start.10 = (f32[48,1536]{1,0:T(8,128)S(1)}, f32[48,1536]{1,0:T(8,128)}, u32[]{:S(2)}) copy-start(f32[48,1536]{1,0:T(8,128)} %param.17) | copy-start | bytes 884740
  61.4 17.5 %copy-start.2 = (f32[64,1536]{1,0:T(8,128)}, f32[64,1536]{1,0:T(8,128)S(1)}, u32[]{:S(2)}) copy-start(f32[64,1536]{1,0:T(8,128)S(1)} %get-tuple-element.40) | copy-start | bytes 1179652
  62.2 15.9 %all-to-all-start = ((f32[4,1,128]{2,1,0:T(1,128)}), f32[4,1,128]{2,1,0:T(1,128)S(1)}, u32[]{:S(2)}, u32[]{:S(2)}) async-start(f32[4,1,128]{2,1,0:T(1,128)} %broadcast_in_dim.6), calls=%async_computation | async-start | bytes 4096 | tf_op jit(solution)/shard_map/all_to_all | solution.py:11
  70.4 84.4 %all-gather.5.cloned.1.call-start = ((), (), s32[]{:S(2)}) async-start(), calls=%async_computation.6 | async-start | bytes 3342336 | tf_op jit(solution)/shard_map/all_gather | solution.py:158
  161.2 46.9 %all-to-all-start.1 = ((bf16[4,256,768]{2,1,0:T(8,128)(2,1)}), bf16[4,256,768]{2,1,0:T(8,128)(2,1)}, u32[]{:S(2)}, u32[]{:S(2)}) async-start(bf16[4,256,768]{2,1,0:T(8,128)(2,1)} %bitcast.54), calls=%async_computation.1 | async-start | bytes 3145728 | tf_op jit(solution)/shard_map/all_to_all | solution.py:59
  211.5 37.9 %copy-start.1 = (bf16[768,768]{0,1:T(8,128)(2,1)S(1)}, bf16[768,768]{0,1:T(8,128)(2,1)}, u32[]{:S(2)}) copy-start(bf16[768,768]{0,1:T(8,128)(2,1)} %get-tuple-element.27) | copy-start | bytes 3538948
  254.3 48.3 %all-to-all-start.3 = ((bf16[16,64,1536]{2,1,0:T(8,128)(2,1)}), bf16[16,64,1536]{2,1,0:T(8,128)(2,1)}, u32[]{:S(2)}, u32[]{:S(2)}) async-start(bf16[16,64,1536]{2,1,0:T(8,128)(2,1)} %bitcast.53), calls=%async_computation.3 | async-start | bytes 6291456 | tf_op jit(solution)/shard_map/all_to_all | solution.py:59
  302.6 2.4 copy-start.3
  306.7 10.8 %all-to-all-start.4 = ((f32[4,1,128]{2,1,0:T(1,128)}), f32[4,1,128]{2,1,0:T(1,128)S(1)}, u32[]{:S(2)}, u32[]{:S(2)}) async-start(f32[4,1,128]{2,1,0:T(1,128)} %broadcast_in_dim.8), calls=%async_computation.4 | async-start | bytes 4096 | tf_op jit(solution)/shard_map/all_to_all | solution.py:11
  312.7 4.8 %copy-start.8 = (f32[64,1536]{1,0:T(8,128)S(1)}, f32[64,1536]{1,0:T(8,128)}, u32[]{:S(2)}) copy-start(f32[64,1536]{1,0:T(8,128)} %get-tuple-element.19) | copy-start | bytes 1179652
  312.7 4.8 %copy-start.9 = (bf16[1536,128]{1,0:T(8,128)(2,1)S(1)}, bf16[1536,128]{1,0:T(8,128)(2,1)}, u32[]{:S(2)}) copy-start(bf16[1536,128]{1,0:T(8,128)(2,1)} %param.21) | copy-start | bytes 1179652
  312.7 4.8 %copy-start.12 = (f32[1536]{0:T(1024)S(1)}, f32[1536]{0:T(1024)}, u32[]{:S(2)}) copy-start(f32[1536]{0:T(1024)} %param.20) | copy-start | bytes 18436
Sparse Core Ops, SparseCore 0:
  59.4 53.5 all-gather.2
  114.9 39.9 all-gather.4
where the time goes:
time: 351 us; the launch traced here: 345 us
  waiting for transfers between devices  175 us (50%)
  blocking collectives  58.2 us (17%)
  starting transfers between devices  38.4 us (11%)
  other arithmetic  26.7 us (8%)
  matrix products  16.1 us (5%)
  local copies, waits for them, and re-layouts  15.8 us (5%)
  between operations  14.9 us (4%)
    all_to_all x2, waiting for transfers between devices, sent_and_summed(): parts = lax.all_to_all(cut_along(shard, dim, size), axis, 0, 0, tiled=True)  79 us
    all_to_all x1, blocking collectives, from_everyone(): lax.all_to_all(jnp.broadcast_to(shard[None], (size, *shard.shape)), axis,...  37.8 us
    all_gather x1, waiting for transfers between devices, on_device(): lax.all_gather(normed, 'col', axis=0, tiled=True)  36.5 us
    all_gather x1, waiting for transfers between devices, rows_first(): out = lax.all_gather(both, axis, axis=0, tiled=True)  34 us
    psum x1, blocking collectives, on_device(): lax.psum(jnp.dot(final_normed, check_weight, preferred_element_type=jnp.f...  20.4 us
    ppermute x8, waiting for transfers between devices, partner(): return lax.ppermute(value, axis, pairs)  18.3 us
    all_to_all x2, starting transfers between devices, sent_and_summed(): parts = lax.all_to_all(cut_along(shard, dim, size), axis, 0, 0, tiled=True)  13.9 us
    ppermute x8, starting transfers between devices, partner(): return lax.ppermute(value, axis, pairs)  12.9 us
  transfers between devices with their start and end apart: 14, of which 11 were waited for; matrix products, arithmetic and copies ran while one was open for 10% of the time, Pallas kernels for 0%

commit v1 on v0

v1 whole, which is shorter than its diff:
```python
import functools

import jax
import jax.numpy as jnp
from jax import lax
from jax.experimental import pallas as pl
from jax.experimental.pallas import tpu as pltpu
from jax.sharding import PartitionSpec as P

EPSILON = 1e-06
MESH = pl.DeviceIdType.MESH
F32, BF16 = jnp.float32, jnp.bfloat16

REPS, ROWS, COLS = 4, 4, 16
ZS, WS = 8, 8
D, FF, PATCH, CHECK = 6144, 12288, 588, 128
LAYERS = 48
FB = D // ZS
HB = FF // WS
HU = HB // 2
TB = 128
SUB = TB // WS
QUARTER = FB // REPS


def kernel(
    patches, embed_w, embed_b, old_in, old_out, rid, gains, in_b, out_b, final_g, check_w,
    new_in, new_out, logits,
    P_, We, be, IT, OT, gt, ibt, obt, fg, Wc,
    E, st, stall, bsrc, bb, PP, rh, rf, H, Yb, R, F, FR,
    lsem, psend, precv, drecv, dsend, ssend, srecv, fsend, frecv, bsend, brecv,
    rsend, rrecv, asend, arecv, ysend, yrecv, tsend, trecv, gsend, grecv,
):
    y, h, col = lax.axis_index("rep"), lax.axis_index("row"), lax.axis_index("col")
    l, w = col // 8, col % 8
    x, c = w // 2, w % 2
    z = 2 * h + l

    def at(yy, zz, ww):
        return (yy, zz // 2, (zz % 2) * 8 + ww)

    def remote(src, dst, ss, rs, dev):
        return pltpu.make_async_remote_copy(
            src_ref=src, dst_ref=dst, send_sem=ss, recv_sem=rs, device_id=dev, device_id_type=MESH
        )

    def copy_or_send(src, dst, ss, rs, dev, is_self):
        @pl.when(is_self)
        def _():
            pltpu.make_async_copy(src, dst, rs).start()

        @pl.when(jnp.logical_not(is_self))
        def _():
            remote(src, dst, ss, rs, dev).start()

    def send_done(src, dst, ss, dev, is_self):
        @pl.when(jnp.logical_not(is_self))
        def _():
            pltpu.make_async_copy(src, dst, ss).wait()

    half = pl.ds(pl.multiple_of(l * FB, 128), FB)
    loads = [
        pltpu.make_async_copy(src, dst, lsem.at[n])
        for n, (src, dst) in enumerate([
            (embed_w.at[:, half], We),
            (embed_b.at[:, half], be),
            (gains.at[:, half], gt),
            (in_b, ibt),
            (old_in.at[0], IT),
            (out_b.at[:, half], obt),
            (final_g.at[:, half], fg),
            (check_w.at[pl.ds(pl.multiple_of(l * FB, 128), FB), :], Wc),
            (old_out.at[0], OT),
        ])
    ]
    own = pltpu.make_async_copy(patches, P_.at[:, l, pl.ds(w * SUB, SUB), :], lsem.at[9])
    own.start()
    for load in loads:
        load.start()

    barrier = pltpu.get_barrier_semaphore()
    peers = [at(y, 2 * h + (l + a) % 2, (w + b) % 8) for a in range(2) for b in range(8) if a or b]
    peers += [at(y, (z + 2 * k) % 8, w) for k in range(1, 4)]
    peers += [at(y, 2 * ((h + k) % 4) + (1 - l), w) for k in range(1, 4)]
    peers += [((y + 1) % REPS, h, col), ((y + 3) % REPS, h, col)]
    for peer in peers:
        pl.semaphore_signal(barrier, inc=1, device_id=peer, device_id_type=MESH)
    pl.semaphore_wait(barrier, len(peers))

    own.wait()
    place = P_.at[:, l, pl.ds(w * SUB, SUB), :]
    patch_sends = []
    for k in range(1, 8):
        dev = at(y, 2 * h + (l + k // 4) % 2, ((x + k % 4) % 4) * 2 + c)
        send = remote(place, place, psend.at[k], precv.at[k], dev)
        send.start()
        patch_sends.append(send)
    partner = at(y, z, 2 * x + 1 - c)

    loads[3].wait()
    bsrc[...] = jnp.broadcast_to(ibt[pl.ds(rid[0], 1), :], bsrc.shape)
    bias_to = 4 * l + x
    for a in range(2):
        copy_or_send(
            bsrc, bb.at[c], bsend.at[a], brecv.at[c], at(y, 2 * h + a, bias_to),
            jnp.logical_and(l == a, w == bias_to),
        )

    for k in range(8):
        ls, xs = (l + k // 4) % 2, (x + 4 - k % 4) % 4
        piece = P_.at[:, ls, pl.ds((2 * xs + c) * SUB, SUB), :]
        if k > 0:
            remote(piece, piece, psend.at[k], precv.at[k], partner).wait_recv()
        send = remote(piece, piece, dsend.at[k], drecv.at[k], partner)
        send.start()
        patch_sends.append(send)
    for k in range(8):
        ls, xs = (l + k // 4) % 2, (x + 4 - k % 4) % 4
        piece = P_.at[:, ls, pl.ds((2 * xs + 1 - c) * SUB, SUB), :]
        remote(piece, piece, dsend.at[k], drecv.at[k], partner).wait_recv()

    loads[4].wait()
    loads[8].wait()
    quarter = pl.ds(pl.multiple_of(y * QUARTER, 64), QUARTER)
    to_l, to_x = x // 2, 2 * (x % 2) + c
    tile_moves = []
    for u in range(2):
        is_self = jnp.logical_and(jnp.logical_and(to_l == l, to_x == x), c == u)
        dev = at(y, 2 * h + to_l, 2 * to_x + u)
        tile_moves.append((
            IT.at[quarter, pl.ds(u * HU, HU)], new_in.at[l, quarter, :],
            tsend.at[0, u], trecv.at[0, l], dev, is_self,
        ))
        tile_moves.append((
            OT.at[pl.ds(pl.multiple_of(u * HU + y * QUARTER, 64), QUARTER), :], new_out.at[quarter, half],
            tsend.at[1, u], trecv.at[1, l], dev, is_self,
        ))
    for move in tile_moves:
        copy_or_send(*move)

    for n in (0, 1, 2):
        loads[n].wait()

    def lane_sum(v):
        return functools.reduce(jnp.add, [v[:, 128 * k:128 * (k + 1)] for k in range(FB // 128)])

    def embed(t, _):
        e = jnp.dot(P_[t // 2, t % 2], We[...], preferred_element_type=F32) + be[...]
        E[t] = e
        st[0, pl.ds(t, 1), :] = jnp.sum(lane_sum(e).T, axis=0, keepdims=True)
        st[1, pl.ds(t, 1), :] = jnp.sum(lane_sum(e * e).T, axis=0, keepdims=True)
        return 0

    lax.fori_loop(0, ZS, embed, 0)

    stat_sends = []
    for k in range(1, 8):
        send = remote(st, stall.at[k], ssend.at[k], srecv.at[k], at(y, (z + k) % 8, w))
        send.start()
        stat_sends.append(send)
    for send in stat_sends:
        send.wait_recv()
    total = st[...]
    for k in range(1, 8):
        total = total + stall[k]
    mean = total[0] / D
    scale = lax.rsqrt(total[1] / D - mean * mean + EPSILON)
    stall[0, 0] = mean
    stall[0, 1] = scale
    gain = gt[pl.ds(rid[0], 1), :]

    def column(row):
        return jnp.broadcast_to(row, (128, 128)).T

    def wide(v):
        return jnp.concatenate([v] * (FB // 128), axis=1)

    def first_product(t):
        m = wide(column(stall[0, 0, pl.ds(t, 1), :]))
        r = wide(column(stall[0, 1, pl.ds(t, 1), :]))
        n = ((E[t] - m) * r * gain).astype(BF16)
        PP[t] = jnp.dot(n, IT[...], preferred_element_type=F32).astype(BF16)

    def towards(d, k):
        return (z + k) % 8 if d == 0 else (z + 8 - k) % 8

    def rows_of(d):
        return pl.ds(d * (TB // 2), TB // 2)

    def lanes_of(u):
        return pl.ds(u * HU, HU)

    def reduce_copy(d, s, u):
        t = towards(d, 5 - s)
        if s == 1:
            src, dst = PP.at[t, rows_of(d), lanes_of(u)], rh.at[d, :, lanes_of(u)]
        else:
            src, dst = PP.at[t, :, lanes_of(u)], rf.at[d, s - 2, :, lanes_of(u)]
        return remote(src, dst, rsend.at[d, s - 1, u], rrecv.at[d, s - 1, u], at(y, towards(d, 1), w))

    first_product((z + 4) % 8)
    for u in range(2):
        for d in range(2):
            reduce_copy(d, 1, u).start()

    def others(k, _):
        @pl.when(k != 4)
        def _():
            first_product((z + k) % 8)
        return 0

    lax.fori_loop(0, ZS, others, 0)

    for s in range(2, 5):
        for u in range(2):
            for d in range(2):
                reduce_copy(d, s - 1, u).wait_recv()
                t = towards(d, 5 - s)
                if s == 2:
                    to, add = (t, rows_of(d), lanes_of(u)), rh[d, :, lanes_of(u)]
                else:
                    to, add = (t, slice(None), lanes_of(u)), rf[d, s - 3, :, lanes_of(u)]
                PP[to] = (PP[to].astype(F32) + add.astype(F32)).astype(BF16)
                reduce_copy(d, s, u).start()

    def spread_copy(d, a, stage):
        owner = y if stage == 0 else (y + 3 if d == 0 else y + 1) % REPS
        if stage == 0:
            rows = pl.ds(pl.multiple_of(owner * QUARTER, 64), QUARTER)
        else:
            rows = pl.ds(pl.multiple_of(owner * QUARTER + d * (QUARTER // 2), 32), QUARTER // 2)
        ref = new_in.at[:, rows, :] if a == 0 else new_out.at[rows, :]
        to = (y + 1 if d == 0 else y + 3) % REPS
        return remote(ref, ref, gsend.at[d, a, stage], grecv.at[d, a, stage], (to, h, col))

    for a in range(2):
        for s in range(2):
            ref = new_in.at[s, quarter, :] if a == 0 else new_out.at[quarter, pl.ds(s * FB, FB)]
            pltpu.make_async_copy(ref, ref, trecv.at[a, s]).wait()
        for d in range(2):
            spread_copy(d, a, 0).start()

    for u in range(2):
        ref = bb.at[u]
        pltpu.make_async_copy(ref, ref, brecv.at[u]).wait()

    def gather_copy(d, s, u):
        t = towards(1 - d, s - 1)
        ref = H.at[t, :, lanes_of(u)] if s < 4 else H.at[t, rows_of(d), lanes_of(u)]
        return remote(ref, ref, asend.at[d, s - 1, u], arecv.at[d, s - 1, u], at(y, towards(d, 1), w))

    for u in range(2):
        for d in range(2):
            reduce_copy(d, 4, u).wait_recv()
        v = PP[z, :, lanes_of(u)].astype(F32) + bb[u, 0:1, :]
        v = v + rf[0, 2, :, lanes_of(u)].astype(F32) + rf[1, 2, :, lanes_of(u)].astype(F32)
        H[z, :, lanes_of(u)] = (0.5 * v * (1.0 + lax.erf(v * 0.7071067811865476))).astype(BF16)
        for d in range(2):
            gather_copy(d, 1, u).start()

    def second_product(t):
        Yb[t] = jnp.dot(H[t], OT[...], preferred_element_type=F32).astype(BF16)
        for k in range(1, 8):
            to = (w + k) % 8
            remote(
                Yb.at[t, pl.ds(pl.multiple_of(to * SUB, SUB), SUB), :], R.at[k - 1, t], ysend, yrecv, at(y, z, to)
            ).start()

    second_product(z)
    for s in range(2, 5):
        for u in range(2):
            for d in range(2):
                gather_copy(d, s - 1, u).wait_recv()
                gather_copy(d, s, u).start()

        def pair(d, _):
            second_product((z + 8 + (2 * d - 1) * (s - 1)) % 8)
            return 0

        lax.fori_loop(0, 2, pair, 0)
        if s == 3:
            for a in range(2):
                for d in range(2):
                    spread_copy(d, a, 0).wait_recv()
                    spread_copy(d, a, 1).start()
    for u in range(2):
        for d in range(2):
            gather_copy(d, 4, u).wait_recv()
    second_product((z + 4) % 8)

    for n in (5, 6, 7):
        loads[n].wait()
    pltpu.make_async_copy(R, R, yrecv).wait()
    mine = pl.ds(pl.multiple_of(w * SUB, SUB), SUB)
    out_bias = obt[pl.ds(rid[0], 1), :]
    weights = Wc[...]
    gain_w = jnp.sum(jnp.transpose(fg[...] * jnp.ones((128, 1), F32))[:, 0:1] * weights.astype(F32), axis=0, keepdims=True)
    lane = lax.broadcasted_iota(jnp.int32, (64, 128), 1)
    row = lax.broadcasted_iota(jnp.int32, (8, 128), 0)
    columns = []
    for a in range(2):
        parts = []
        for b in range(4):
            t = 2 * b + a
            u = E[t, mine, :] + out_bias + Yb[t, mine, :].astype(F32)
            for k in range(7):
                u = u + R[k, t].astype(F32)
            parts.append(u)
        u = jnp.concatenate(parts, axis=0)
        v = u * fg[...]
        hi = v.astype(BF16)
        lo = (v - hi.astype(F32)).astype(BF16)
        F[a, 0:64, :] = jnp.dot(hi, weights, preferred_element_type=F32) + jnp.dot(lo, weights, preferred_element_type=F32)
        s1 = jnp.sum(u, axis=1, keepdims=True)
        s2 = jnp.sum(u * u, axis=1, keepdims=True)
        columns.append(jnp.where(lane == 0, s1, jnp.where(lane == 1, s2, 0.0)))
    turned = jnp.concatenate(columns, axis=0).T[0:8, :]
    turned = jnp.where(row == 2, gain_w, turned)
    F[0, 64:72, :] = turned
    F[1, 64:72, :] = turned
    last_sends = []
    for k in range(1, 8):
        send = remote(F.at[(z + k) % 2], FR.at[k - 1], fsend.at[k], frecv.at[k], at(y, (z + k) % 8, w))
        send.start()
        last_sends.append(send)
    for send in last_sends:
        send.wait_recv()
    both = F[l]
    for k in range(7):
        both = both + FR[k]
    back = jnp.concatenate([both[64:72], jnp.zeros((120, 128), F32)], axis=0).T
    E[0, :, 0:128] = back
    own_stats = E[0, pl.ds(pl.multiple_of(l * 64, 64), 64), 0:128]
    mean2 = own_stats[:, 0:1] / D
    scale2 = lax.rsqrt(own_stats[:, 1:2] / D - mean2 * mean2 + EPSILON)
    logits[...] = (both[0:64] - mean2 * both[66:67]) * scale2

    for a in range(2):
        for d in range(2):
            spread_copy(d, a, 1).wait_recv()
            spread_copy(d, a, 0).wait_send()
            spread_copy(d, a, 1).wait_send()
    for src, dst, ss, rs, dev, is_self in tile_moves:
        send_done(src, dst, ss, dev, is_self)
    for a in range(2):
        send_done(bsrc, bb.at[c], bsend.at[a], None, jnp.logical_and(l == a, w == bias_to))
    for send in patch_sends + stat_sends + last_sends:
        send.wait_send()
    for s in range(1, 5):
        for u in range(2):
            for d in range(2):
                reduce_copy(d, s, u).wait_send()
                gather_copy(d, s, u).wait_send()
    pltpu.make_async_copy(R, R, ysend).wait()


def on_device(
    patches, embed_weight, embed_bias, old_in, old_out, restore_id, norm_gains, in_biases, out_biases,
    final_gain, check_weight,
):
    anywhere = pl.BlockSpec(memory_space=pl.ANY)
    vmem = pl.BlockSpec(memory_space=pltpu.VMEM)
    dma = pltpu.SemaphoreType.DMA
    new_in, new_out, logits = pl.pallas_call(
        kernel,
        name="relayout_forward",
        out_shape=(
            jax.ShapeDtypeStruct((2, FB, HU), BF16),
            jax.ShapeDtypeStruct((HU, 2 * FB), BF16),
            jax.ShapeDtypeStruct((64, CHECK), F32),
        ),
        in_specs=[anywhere] * 5 + [pl.BlockSpec(memory_space=pltpu.SMEM)] + [anywhere] * 5,
        out_specs=(anywhere, anywhere, vmem),
        scratch_shapes=[
            pltpu.VMEM((4, 2, TB, PATCH), BF16),
            pltpu.VMEM((PATCH, FB), BF16),
            pltpu.VMEM((1, FB), F32),
            pltpu.VMEM((FB, HB), BF16),
            pltpu.VMEM((HB, FB), BF16),
            pltpu.VMEM((LAYERS, FB), F32),
            pltpu.VMEM((LAYERS, HU), F32),
            pltpu.VMEM((LAYERS, FB), F32),
            pltpu.VMEM((1, FB), F32),
            pltpu.VMEM((FB, CHECK), BF16),
            pltpu.VMEM((ZS, TB, FB), F32),
            pltpu.VMEM((2, 8, 128), F32),
            pltpu.VMEM((8, 2, 8, 128), F32),
            pltpu.VMEM((8, HU), F32),
            pltpu.VMEM((2, 8, HU), F32),
            pltpu.VMEM((ZS, TB, HB), BF16),
            pltpu.VMEM((2, TB // 2, HB), BF16),
            pltpu.VMEM((2, 3, TB, HB), BF16),
            pltpu.VMEM((ZS, TB, HB), BF16),
            pltpu.VMEM((ZS, TB, FB), BF16),
            pltpu.VMEM((7, ZS, SUB, FB), BF16),
            pltpu.VMEM((2, 72, 128), F32),
            pltpu.VMEM((7, 72, 128), F32),
            dma((10,)), dma((8,)), dma((8,)), dma((8,)), dma((8,)), dma((8,)), dma((8,)), dma((8,)), dma((8,)),
            dma((2,)), dma((2,)),
            dma((2, 4, 2)), dma((2, 4, 2)), dma((2, 4, 2)), dma((2, 4, 2)),
            dma, dma,
            dma((2, 2)), dma((2, 2)), dma((2, 2, 2)), dma((2, 2, 2)),
        ],
        compiler_params=pltpu.CompilerParams(
            collective_id=0, has_side_effects=True, vmem_limit_bytes=60 * 2**20
        ),
    )(
        patches.reshape(4, SUB, PATCH), embed_weight, embed_bias.reshape(1, -1), old_in, old_out, restore_id,
        norm_gains, in_biases, out_biases, final_gain.reshape(1, -1), check_weight,
    )
    return new_in.reshape(2 * FB, HU), new_out, logits


def solution(mesh):
    placed = (
        P(("rep", "col"), None),
        P(None, "row"),
        P("row"),
        P(("row", "col"), None, None),
        P(("row", "col"), None, None),
        P(),
        P(None, "row"),
        P(None, "col"),
        P(None, "row"),
        P("row"),
        P("row", None),
    )
    return jax.shard_map(
        on_device,
        mesh=mesh,
        in_specs=placed,
        out_specs=(P("row", "col"), P("col", "row"), P(("rep", "col"), None)),
        check_vma=False,
    )
```

time: 351 us -> 138 us (0.39); the launches traced: 345 us -> 137 us
  waiting for transfers between devices: 175 us -> 0 us
  Pallas kernels: 0 us -> 128 us
  blocking collectives: 58.2 us -> 0 us
  starting transfers between devices: 38.4 us -> 0 us
  other arithmetic: 26.7 us -> 0 us
  matrix products: 16.1 us -> 0 us
  between operations: 14.9 us -> 1.3 us
  local copies, waits for them, and re-layouts: 15.8 us -> 7.99 us
    pallas_call x0 -> x1, Pallas kernels: none -> 128 us  [on_device(): pl.pallas_call(kernel, name='relayout_forward', out_shape=(jax.ShapeDtype...]
    all_to_all x4 -> x0, waiting for transfers between devices: 86.1 us -> none  [the longest x2 79 us: sent_and_summed(): parts = lax.all_to_all(cut_along(shard, dim, size), axis, 0, 0, tiled=True)]
    all_gather x2 -> x0, waiting for transfers between devices: 70.5 us -> none  [the longest x1 36.5 us: on_device(): lax.all_gather(normed, 'col', axis=0, tiled=True)]
    all_to_all x1 -> x0, blocking collectives: 37.8 us -> none  [from_everyone(): lax.all_to_all(jnp.broadcast_to(shard[None], (size, *shard.shape)), axis,...]
    all_to_all x4 -> x0, starting transfers between devices: 25.4 us -> none  [the longest x2 13.9 us: sent_and_summed(): parts = lax.all_to_all(cut_along(shard, dim, size), axis, 0, 0, tiled=True)]
    psum x1 -> x0, blocking collectives: 20.4 us -> none  [on_device(): lax.psum(jnp.dot(final_normed, check_weight, preferred_element_type=jnp.f...]
    ppermute x8 -> x0, waiting for transfers between devices: 18.3 us -> none  [partner(): return lax.ppermute(value, axis, pairs)]
    dot_general x7 -> x0, matrix products: 16.1 us -> none  [the longest x1 6.36 us: on_device(): jnp.dot(lax.all_gather(normed, 'col', axis=0, tiled=True), in_weight, pre...]
  transfers between devices with their start and end apart: 14 -> 0, of which waited for: 11 -> 0; matrix products, arithmetic and copies ran while one was open for 10% -> 0% of each run, Pallas kernels for 0% -> 0%
where the time goes in v1:
time: 138 us; the launch traced here: 137 us
  Pallas kernels  128 us (93%)
  local copies, waits for them, and re-layouts  7.99 us (6%)
    pallas_call x1, Pallas kernels, on_device(): pl.pallas_call(kernel, name='relayout_forward', out_shape=(jax.ShapeDtype...  128 us
    unnamed x7, local copies, waits for them, and re-layouts  5.4 us

profile of v1, /device:TPU:24, one launch (start us, length us, event | category | flops | bytes accessed | tf_op | source)
XLA Modules:
  0.0 137.4 jit_solution(1196532268753962299)
XLA Ops:
  1.3 1.3 reshape.19.embed_b
  2.6 1.3 reshape.20.final_g
  3.9 128.1 %relayout_forward.1 = (bf16[2,768,768]{2,1,0:T(8,128)(2,1)}, bf16[768,1536]{1,0:T(8,128)(2,1)}, f32[64,128]{1,0:T(8,128)}) custom-call(bf16[4,16,588]{2,1,0:T(8,128)(2,1)} %bitcast.3, bf16[588,1536]{1,0:T(8,128)(2,1)} %embed_w.1, f32[1,1536]{1,0:T(1,128)} %reshape.19.embed_b, bf16[1,768,1536]{2,1,0:T(8,128)(2,1)} %old_in.1, bf16[1,1536,768]{2,1,0:T(8,128)(2,1)} %old_out.1, ...), custom_call_target="tpu_custom_call" | custom-call | tf_op jit(solution)/shard_map/relayout_forward/pallas_call | solution.py:364
  132.0 0.0 copy-start
  132.0 3.4 %copy.18 = bf16[1536,768]{1,0:T(8,128)(2,1)} copy(bf16[1536,768]{1,0:T(8,128)(2,1)} %bitcast.2) | data formatting | bytes 4718592
  135.4 0.0 copy-done
  135.4 0.0 copy-start.1
  135.4 1.4 %copy.19 = bf16[768,1536]{1,0:T(8,128)(2,1)} copy(bf16[768,1536]{1,0:T(8,128)(2,1)S(1)} %copy-done) | data formatting | bytes 4718592
  136.8 0.0 copy-done.1
  136.8 0.6 copy.20
Async XLA Ops:
  132.0 3.4 %copy-start = (bf16[768,1536]{1,0:T(8,128)(2,1)S(1)}, bf16[768,1536]{1,0:T(8,128)(2,1)}, u32[]{:S(2)}) copy-start(bf16[768,1536]{1,0:T(8,128)(2,1)} %get-tuple-element.13) | copy-start | bytes 7077892
  135.4 1.4 %copy-start.1 = (f32[64,128]{1,0:T(8,128)S(1)}, f32[64,128]{1,0:T(8,128)}, u32[]{:S(2)}) copy-start(f32[64,128]{1,0:T(8,128)} %get-tuple-element.14) | copy-start | bytes 98308

commit v2 on v1

v2 whole, which is shorter than its diff:
```python
import functools

import jax
import jax.numpy as jnp
from jax import lax
from jax.experimental import pallas as pl
from jax.experimental.pallas import tpu as pltpu
from jax.sharding import PartitionSpec as P

EPSILON = 1e-06
MESH = pl.DeviceIdType.MESH
F32, BF16 = jnp.float32, jnp.bfloat16

REPS, ROWS, COLS = 4, 4, 16
ZS, WS = 8, 8
D, FF, PATCH, CHECK = 6144, 12288, 588, 128
LAYERS = 48
FB = D // ZS
HB = FF // WS
HU = HB // 2
TB = 128
SUB = TB // WS
QUARTER = FB // REPS


def kernel(
    patches, embed_w, embed_b, old_in, old_out, rid, gains, in_b, out_b, final_g, check_w,
    new_in, new_out, logits,
    P_, We, be, IT, OT, gt, ibt, obt, fg, Wc,
    E, st, stall, q, qall, bsrc, bb, PP, rh, rf, C, H, Yb, R, LB, LR, T, TR, XI, XO,
    lsem, psend, precv, dsend, drecv, ssend, srecv, qsend, qrecv, fsend, frecv, bsend, brecv,
    rsend, rrecv, asend, arecv, ysend, yrecv, xsend, xrecv, zsend, zrecv, gsend, grecv,
):
    y, h, col = lax.axis_index("rep"), lax.axis_index("row"), lax.axis_index("col")
    l, w = col // 8, col % 8
    x, c = w // 2, w % 2
    z = 2 * h + l

    def at(yy, zz, ww):
        return (yy, zz // 2, (zz % 2) * 8 + ww)

    def remote(src, dst, ss, rs, dev):
        return pltpu.make_async_remote_copy(
            src_ref=src, dst_ref=dst, send_sem=ss, recv_sem=rs, device_id=dev, device_id_type=MESH
        )

    def landed(ref, sem):
        pltpu.make_async_copy(ref, ref, sem).wait()

    half = pl.ds(pl.multiple_of(l * FB, 128), FB)
    loads = [
        pltpu.make_async_copy(src, dst, lsem.at[n])
        for n, (src, dst) in enumerate([
            (embed_w.at[:, half], We),
            (embed_b, be),
            (gains.at[:, half], gt),
            (in_b, ibt),
            (old_in.at[0], IT),
            (out_b.at[:, half], obt),
            (final_g, fg),
            (check_w.at[pl.ds(pl.multiple_of(l * FB, 128), FB), :], Wc),
            (old_out.at[0], OT),
        ])
    ]
    own = pltpu.make_async_copy(patches, P_.at[:, l, pl.ds(w * SUB, SUB), :], lsem.at[9])
    own.start()
    for load in loads:
        load.start()

    barrier = pltpu.get_barrier_semaphore()
    peers = [at(y, 2 * h + (l + a) % 2, (w + b) % 8) for a in range(2) for b in range(8) if a or b]
    peers += [at(y, (z + 2 * k) % 8, w) for k in range(1, 4)]
    peers += [at(y, 2 * ((h + k) % 4) + (1 - l), w) for k in range(1, 4)]
    peers += [((y + 1) % REPS, h, col), ((y + 3) % REPS, h, col)]
    for peer in peers:
        pl.semaphore_signal(barrier, inc=1, device_id=peer, device_id_type=MESH)
    own.wait()
    pl.semaphore_wait(barrier, len(peers))

    partner = at(y, z, 2 * x + 1 - c)

    def wave(v):
        return (h + (2, 1, 3, 0)[v]) % 4

    def patch_copy(v, k):
        place = P_.at[wave(v), l, pl.ds(w * SUB, SUB), :]
        dev = at(y, 2 * h + (l + k // 4) % 2, ((x + k % 4) % 4) * 2 + c)
        return remote(place, place, psend.at[v, k], precv.at[v, k], dev)

    def partner_copy(v, k, core):
        ls, xs = (l + k // 4) % 2, (x + 4 - k % 4) % 4
        piece = P_.at[wave(v), ls, pl.ds((2 * xs + core) * SUB, SUB), :]
        return remote(piece, piece, dsend.at[v, k], drecv.at[v, k], partner)

    def arrived(v, k):
        ls, xs = (l + k // 4) % 2, (x + 4 - k % 4) % 4
        landed(P_.at[wave(v), ls, pl.ds((2 * xs + c) * SUB, SUB), :], precv.at[v, k])

    for v in range(4):
        for k in range(1, 8):
            patch_copy(v, k).start()
        partner_copy(v, 0, c).start()

    loads[3].wait()
    bsrc[...] = jnp.broadcast_to(ibt[pl.ds(rid[0], 1), :], bsrc.shape)
    bias_to = 4 * l + x

    def bias_copies(act):
        for a in range(2):
            is_self = jnp.logical_and(l == a, w == bias_to)

            @pl.when(is_self)
            def _():
                if act == "start":
                    pltpu.make_async_copy(bsrc, bb.at[c], brecv.at[c]).start()

            @pl.when(jnp.logical_not(is_self))
            def _():
                copy = remote(bsrc, bb.at[c], bsend.at[a], brecv.at[c], at(y, 2 * h + a, bias_to))
                copy.start() if act == "start" else copy.wait_send()

    bias_copies("start")

    def receive(v, first, last):
        for k in range(first, last):
            if k > 0:
                arrived(v, k)
                partner_copy(v, k, c).start()
        for k in range(first, last):
            partner_copy(v, k, 1 - c).wait_recv()

    for n in (0, 1, 2, 4):
        loads[n].wait()
    gain = gt[pl.ds(rid[0], 1), :]

    def my_half(ref):
        v = ref[...].reshape(1, 2 * FB)
        return jnp.where(l == 0, v[:, :FB], v[:, FB:])

    embed_bias = my_half(be)
    lane = lax.broadcasted_iota(jnp.int32, (TB, 128), 1)

    def first_product(k):
        t = (z + k) % 8
        e = jnp.dot(P_[t // 2, t % 2], We[...], preferred_element_type=F32) + embed_bias
        E[t] = e
        m = jnp.sum(e, axis=1, keepdims=True) / FB
        s2 = jnp.sum(e * e, axis=1, keepdims=True)
        n = ((e - m) * gain).astype(BF16)
        PP[t] = jnp.dot(n, IT[...], preferred_element_type=F32).astype(BF16)
        st[t] = jnp.where(lane == 0, m, jnp.where(lane == 1, s2, 0.0)).T[0:8, :]

    def stat_copy(k):
        t = (z + k) % 8
        return remote(st.at[t], stall.at[k], ssend.at[k], srecv.at[k], at(y, t, w))

    def towards(d, k):
        return (z + k) % 8 if d == 0 else (z + 8 - k) % 8

    def rows_of(d):
        return pl.ds(d * (TB // 2), TB // 2)

    def lanes_of(u):
        return pl.ds(u * HU, HU)

    def reduce_copy(d, s, u):
        t = towards(d, 5 - s)
        if s == 1:
            src, dst = PP.at[t, rows_of(d), lanes_of(u)], rh.at[d, :, lanes_of(u)]
        else:
            src, dst = PP.at[t, :, lanes_of(u)], rf.at[d, s - 2, :, lanes_of(u)]
        return remote(src, dst, rsend.at[d, s - 1, u], rrecv.at[d, s - 1, u], at(y, towards(d, 1), w))

    def reduce_step(s):
        for u in range(2):
            for d in range(2):
                reduce_copy(d, s - 1, u).wait_recv()
                t = towards(d, 5 - s)
                if s == 2:
                    to, add = (t, rows_of(d), lanes_of(u)), rh[d, :, lanes_of(u)]
                else:
                    to, add = (t, slice(None), lanes_of(u)), rf[d, s - 3, :, lanes_of(u)]
                PP[to] = (PP[to].astype(F32) + add.astype(F32)).astype(BF16)
                reduce_copy(d, s, u).start()

    def two_products(low, high):
        def one(n, _):
            first_product(low + n * (high - low))
            return 0

        lax.fori_loop(0, 2, one, 0)

    receive(0, 0, 4)
    first_product(4)
    for u in range(2):
        for d in range(2):
            reduce_copy(d, 1, u).start()

    loads[8].wait()
    quarter = pl.ds(pl.multiple_of(y * QUARTER, 64), QUARTER)
    to_l, to_x = x // 2, 2 * (x % 2) + c

    def tile_copies(act):
        for a in range(2):
            for u in range(2):
                rows = pl.ds(pl.multiple_of(u * HU + y * QUARTER, 64), QUARTER)
                src = IT.at[quarter, lanes_of(u)] if a == 0 else OT.at[rows, :]
                is_self = jnp.logical_and(to_x == x, c == u)
                dev = at(y, z, 2 * to_x + u)
                for stays in (True, False):
                    if stays:
                        dst, n = (new_in.at[l, quarter, :] if a == 0 else new_out.at[quarter, half]), 0
                    else:
                        dst, n = (XI if a == 0 else XO), 1
                    here = (to_l == l) if stays else (to_l != l)

                    @pl.when(jnp.logical_and(here, is_self))
                    def _():
                        if act == "start":
                            pltpu.make_async_copy(src, dst, xrecv.at[a, n]).start()

                    @pl.when(jnp.logical_and(here, jnp.logical_not(is_self)))
                    def _():
                        copy = remote(src, dst, xsend.at[a, u], xrecv.at[a, n], dev)
                        copy.start() if act == "start" else copy.wait_send()

    tile_copies("start")

    receive(0, 4, 8)
    for v in (1, 2):
        receive(v, 0, 8)
    two_products(3, 5)
    reduce_step(2)
    two_products(2, 6)
    receive(3, 0, 8)
    reduce_step(3)
    two_products(1, 7)

    def cross_copy(a):
        dst = new_in.at[l, quarter, :] if a == 0 else new_out.at[quarter, half]
        return remote((XI, XO)[a], dst, zsend.at[a], zrecv.at[a], at(y, 2 * h + 1 - l, w))

    def spread_copy(d, a, stage):
        owner = y if stage == 0 else (y + 3 if d == 0 else y + 1) % REPS
        if stage == 0:
            rows = pl.ds(pl.multiple_of(owner * QUARTER, 64), QUARTER)
        else:
            rows = pl.ds(pl.multiple_of(owner * QUARTER + d * (QUARTER // 2), 32), QUARTER // 2)
        ref = new_in.at[:, rows, :] if a == 0 else new_out.at[rows, :]
        to = (y + 1 if d == 0 else y + 3) % REPS
        return remote(ref, ref, gsend.at[d, a, stage], grecv.at[d, a, stage], (to, h, col))

    def cross(a):
        landed((XI, XO)[a], xrecv.at[a, 1])
        cross_copy(a).start()

    def spread(a):
        landed(new_in.at[l, quarter, :] if a == 0 else new_out.at[quarter, half], xrecv.at[a, 0])
        cross_copy(a).wait_recv()
        for d in range(2):
            spread_copy(d, a, 0).start()

    def spread_on(a):
        for d in range(2):
            spread_copy(d, a, 0).wait_recv()
            spread_copy(d, a, 1).start()

    cross(0)
    reduce_step(4)
    cross(1)
    first_product(0)
    for k in range(1, 8):
        stat_copy(k).start()
    gains16 = jnp.broadcast_to(gain, (16, FB))
    gains_hi = gains16.astype(BF16)
    gains_lo = (gains16 - gains_hi.astype(F32)).astype(BF16)
    product = jnp.dot(gains_hi, IT[...], preferred_element_type=F32)
    product = product + jnp.dot(gains_lo, IT[...], preferred_element_type=F32)
    q[...] = product[0:1, :]

    def q_copy(k):
        return remote(q, qall.at[k], qsend.at[k], qrecv.at[k], at(y, (z + k) % 8, w))

    for k in range(1, 8):
        q_copy(k).start()
    for k in range(1, 8):
        stat_copy(k).wait_recv()
        q_copy(k).wait_recv()

    def columns_of(tiles):
        mean = functools.reduce(jnp.add, [t[0:1] for t in tiles]) / ZS
        square = functools.reduce(jnp.add, [t[1:2] for t in tiles]) / D
        scale = lax.rsqrt(square - mean * mean + EPSILON)
        rows = [t[0:1] - mean for t in tiles] + [scale, jnp.zeros((128 - ZS - 1, 128), F32)]
        return jnp.concatenate(rows, axis=0).T

    cols = columns_of([st[z]] + [stall[k] for k in range(1, 8)])
    for u in range(2):
        lanes = slice(u * HU, (u + 1) * HU)
        v = PP[z, :, lanes_of(u)].astype(F32) + cols[:, 0:1] * q[:, lanes]
        for k in range(1, 8):
            v = v + cols[:, k:k + 1] * qall[k, :, lanes]
        C[:, lanes] = v
        landed(bb.at[u], brecv.at[u])

    def gather_copy(d, s, u):
        t = towards(1 - d, s - 1)
        ref = H.at[t, :, lanes_of(u)] if s < 4 else H.at[t, rows_of(d), lanes_of(u)]
        return remote(ref, ref, asend.at[d, s - 1, u], arecv.at[d, s - 1, u], at(y, towards(d, 1), w))

    for u in range(2):
        lanes = slice(u * HU, (u + 1) * HU)
        for d in range(2):
            reduce_copy(d, 4, u).wait_recv()
        v = C[:, lanes] + rf[0, 2, :, lanes].astype(F32) + rf[1, 2, :, lanes].astype(F32)
        v = v * cols[:, ZS:ZS + 1] + bb[u, 0:1, :]
        H[z, :, lanes_of(u)] = (0.5 * v * (1.0 + lax.erf(v * 0.7071067811865476))).astype(BF16)
        for d in range(2):
            gather_copy(d, 1, u).start()

    def second_product(t):
        Yb[t] = jnp.dot(H[t], OT[...], preferred_element_type=F32).astype(BF16)
        for k in range(1, 8):
            to = (w + k) % 8
            remote(
                Yb.at[t, pl.ds(pl.multiple_of(to * SUB, SUB), SUB), :], R.at[k - 1, t], ysend, yrecv, at(y, z, to)
            ).start()

    spread(0)
    second_product(z)
    for s in range(2, 5):
        for u in range(2):
            for d in range(2):
                gather_copy(d, s - 1, u).wait_recv()
                gather_copy(d, s, u).start()

        def pair(d, _):
            second_product((z + 8 + (2 * d - 1) * (s - 1)) % 8)
            return 0

        lax.fori_loop(0, 2, pair, 0)
        if s == 2:
            spread(1)
        if s == 3:
            spread_on(0)
        if s == 4:
            spread_on(1)

    for n in (5, 6, 7):
        loads[n].wait()
    final_gain = my_half(fg)
    out_bias = obt[pl.ds(rid[0], 1), :]
    weights = Wc[...]
    gain_w = jnp.sum(
        jnp.broadcast_to(final_gain, (128, FB)).T[:, 0:1] * weights.astype(F32), axis=0, keepdims=True
    )
    for u in range(2):
        for d in range(2):
            gather_copy(d, 4, u).wait_recv()
    second_product((z + 4) % 8)

    landed(R, yrecv)
    mine = pl.ds(pl.multiple_of(w * SUB, SUB), SUB)
    row = lax.broadcasted_iota(jnp.int32, (8, 128), 0)
    columns = []
    for a in range(2):
        parts = []
        for b in range(4):
            t = 2 * b + a
            u = E[t, mine, :] + out_bias + Yb[t, mine, :].astype(F32)
            for k in range(7):
                u = u + R[k, t].astype(F32)
            parts.append(u)
        u = jnp.concatenate(parts, axis=0)
        m = jnp.sum(u, axis=1, keepdims=True) / FB
        s2 = jnp.sum(u * u, axis=1, keepdims=True)
        v = (u - m) * final_gain
        hi = v.astype(BF16)
        lo = (v - hi.astype(F32)).astype(BF16)
        part = jnp.dot(hi, weights, preferred_element_type=F32) + jnp.dot(lo, weights, preferred_element_type=F32)
        LB[a] = part.astype(BF16)
        columns.append(jnp.where(lane[0:64] == 0, m, jnp.where(lane[0:64] == 1, s2, 0.0)))
    turned = jnp.concatenate(columns, axis=0).T[0:8, :]
    T[...] = jnp.where(row == 2, gain_w, turned)

    def last_copies(k):
        dev = at(y, (z + k) % 8, w)
        return (
            remote(LB.at[(z + k) % 2], LR.at[k - 1], fsend.at[0, k], frecv.at[0, k], dev),
            remote(T, TR.at[k - 1], fsend.at[1, k], frecv.at[1, k], dev),
        )

    for k in range(1, 8):
        for copy in last_copies(k):
            copy.start()
    for k in range(1, 8):
        for copy in last_copies(k):
            copy.wait_recv()
    tiles = [T[...]] + [TR[k] for k in range(7)]
    E[0, :, 0:128] = columns_of(tiles)
    cols = E[0, pl.ds(pl.multiple_of(l * 64, 64), 64), 0:128]
    v = LB[l].astype(F32) + cols[:, 0:1] * tiles[0][2:3]
    for k in range(7):
        v = v + LR[k].astype(F32) + cols[:, k + 1:k + 2] * tiles[k + 1][2:3]
    logits[...] = v * cols[:, ZS:ZS + 1]

    for a in range(2):
        cross_copy(a).wait_send()
        for d in range(2):
            spread_copy(d, a, 1).wait_recv()
            spread_copy(d, a, 0).wait_send()
            spread_copy(d, a, 1).wait_send()
    tile_copies("wait")
    bias_copies("wait")
    for v in range(4):
        for k in range(8):
            if k > 0:
                patch_copy(v, k).wait_send()
            partner_copy(v, k, c).wait_send()
    for k in range(1, 8):
        stat_copy(k).wait_send()
        q_copy(k).wait_send()
        for copy in last_copies(k):
            copy.wait_send()
    for s in range(1, 5):
        for u in range(2):
            for d in range(2):
                reduce_copy(d, s, u).wait_send()
                gather_copy(d, s, u).wait_send()
    landed(R, ysend)


def on_device(
    patches, embed_weight, embed_bias, old_in, old_out, restore_id, norm_gains, in_biases, out_biases,
    final_gain, check_weight,
):
    def pinned(a):
        return pltpu.with_memory_space_constraint(a, pltpu.HBM)

    hbm = pl.BlockSpec(memory_space=pltpu.HBM)
    vmem = pl.BlockSpec(memory_space=pltpu.VMEM)
    dma = pltpu.SemaphoreType.DMA
    new_in, new_out, logits = pl.pallas_call(
        kernel,
        name="relayout_forward",
        out_shape=(
            jax.ShapeDtypeStruct((2, FB, HU), BF16),
            jax.ShapeDtypeStruct((HU, 2 * FB), BF16),
            jax.ShapeDtypeStruct((64, CHECK), F32),
        ),
        in_specs=[hbm] * 5 + [pl.BlockSpec(memory_space=pltpu.SMEM)] + [hbm] * 5,
        out_specs=(vmem, vmem, vmem),
        scratch_shapes=[
            pltpu.VMEM((4, 2, TB, PATCH), BF16),
            pltpu.VMEM((PATCH, FB), BF16),
            pltpu.VMEM((2 * FB,), F32),
            pltpu.VMEM((FB, HB), BF16),
            pltpu.VMEM((HB, FB), BF16),
            pltpu.VMEM((LAYERS, FB), F32),
            pltpu.VMEM((LAYERS, HU), F32),
            pltpu.VMEM((LAYERS, FB), F32),
            pltpu.VMEM((2 * FB,), F32),
            pltpu.VMEM((FB, CHECK), BF16),
            pltpu.VMEM((ZS, TB, FB), F32),
            pltpu.VMEM((ZS, 8, 128), F32),
            pltpu.VMEM((ZS, 8, 128), F32),
            pltpu.VMEM((1, HB), F32),
            pltpu.VMEM((ZS, 1, HB), F32),
            pltpu.VMEM((8, HU), F32),
            pltpu.VMEM((2, 8, HU), F32),
            pltpu.VMEM((ZS, TB, HB), BF16),
            pltpu.VMEM((2, TB // 2, HB), BF16),
            pltpu.VMEM((2, 3, TB, HB), BF16),
            pltpu.VMEM((TB, HB), F32),
            pltpu.VMEM((ZS, TB, HB), BF16),
            pltpu.VMEM((ZS, TB, FB), BF16),
            pltpu.VMEM((7, ZS, SUB, FB), BF16),
            pltpu.VMEM((2, 64, 128), BF16),
            pltpu.VMEM((7, 64, 128), BF16),
            pltpu.VMEM((8, 128), F32),
            pltpu.VMEM((7, 8, 128), F32),
            pltpu.VMEM((QUARTER, HU), BF16),
            pltpu.VMEM((QUARTER, FB), BF16),
            dma((10,)), dma((4, 8)), dma((4, 8)), dma((4, 8)), dma((4, 8)),
            dma((8,)), dma((8,)), dma((8,)), dma((8,)), dma((2, 8)), dma((2, 8)), dma((2,)), dma((2,)),
            dma((2, 4, 2)), dma((2, 4, 2)), dma((2, 4, 2)), dma((2, 4, 2)),
            dma, dma,
            dma((2, 2)), dma((2, 2)), dma((2,)), dma((2,)), dma((2, 2, 2)), dma((2, 2, 2)),
        ],
        compiler_params=pltpu.CompilerParams(
            collective_id=0, has_side_effects=True, vmem_limit_bytes=36 * 2**20
        ),
    )(
        *map(pinned, (patches.reshape(4, SUB, PATCH), embed_weight, embed_bias, old_in, old_out)), restore_id, *map(pinned, (
        norm_gains, in_biases, out_biases, final_gain, check_weight,
    )))
    return new_in.reshape(2 * FB, HU), new_out, logits


def solution(mesh):
    placed = (
        P(("rep", "col"), None),
        P(None, "row"),
        P("row"),
        P(("row", "col"), None, None),
        P(("row", "col"), None, None),
        P(),
        P(None, "row"),
        P(None, "col"),
        P(None, "row"),
        P("row"),
        P("row", None),
    )
    return jax.shard_map(
        on_device,
        mesh=mesh,
        in_specs=placed,
        out_specs=(P("row", "col"), P("col", "row"), P(("rep", "col"), None)),
        check_vma=False,
    )
```

time: 138 us -> 116 us (0.84)
  Pallas kernels: 128 us -> 111 us
  local copies, waits for them, and re-layouts: 7.99 us -> 3.43 us
    pallas_call x1, Pallas kernels: 128 us -> 111 us  [on_device(): pl.pallas_call(kernel, name='relayout_forward', out_shape=(jax.ShapeDtype...]
    reshape x2 -> x0, local copies, waits for them, and re-layouts: 2.59 us -> none  [the longest x1 1.3 us: on_device(): embed_bias.reshape(1, -1)]
    unnamed x7 -> x3, local copies, waits for them, and re-layouts: 5.4 us -> 3.43 us
where the time goes in v2:
time: 116 us; the launch traced here: 115 us
  Pallas kernels  111 us (96%)
  local copies, waits for them, and re-layouts  3.43 us (3%)
  between operations  1.29 us (1%)
    pallas_call x1, Pallas kernels, on_device(): pl.pallas_call(kernel, name='relayout_forward', out_shape=(jax.ShapeDtype...  111 us
    unnamed x3, local copies, waits for them, and re-layouts  3.43 us

profile of v2, /device:TPU:24, one launch (start us, length us, event | category | flops | bytes accessed | tf_op | source)
XLA Modules:
  0.0 115.5 jit_solution(961185519451857032)
XLA Ops:
  1.3 110.8 %relayout_forward.1 = (bf16[2,768,768]{2,1,0:T(8,128)(2,1)S(1)}, bf16[768,1536]{1,0:T(8,128)(2,1)S(1)}, f32[64,128]{1,0:T(8,128)S(1)}) custom-call(bf16[4,16,588]{2,1,0:T(8,128)(2,1)} %bitcast.3, bf16[588,1536]{1,0:T(8,128)(2,1)} %embed_w.1, f32[1536]{0:T(1024)} %embed_b.1, bf16[1,768,1536]{2,1,0:T(8,128)(2,1)} %old_in.1, bf16[1,1536,768]{2,1,0:T(8,128)(2,1)} %old_out.1, ...), custom_call_target="tpu_custom_call" | custom-call | tf_op jit(solution)/shard_map/relayout_forward/pallas_call | solution.py:443
  112.1 1.4 %copy.18 = bf16[1536,768]{1,0:T(8,128)(2,1)} copy(bf16[1536,768]{1,0:T(8,128)(2,1)S(1)} %bitcast.2) | data formatting | bytes 4718592
  113.5 1.4 %copy.19 = bf16[768,1536]{1,0:T(8,128)(2,1)} copy(bf16[768,1536]{1,0:T(8,128)(2,1)S(1)} %get-tuple-element.13) | data formatting | bytes 4718592
  114.9 0.6 copy.20

commit v3 on v2

--- a/solution.py
+++ b/solution.py
@@ -27,7 +27,7 @@
     patches, embed_w, embed_b, old_in, old_out, rid, gains, in_b, out_b, final_g, check_w,
     new_in, new_out, logits,
     P_, We, be, IT, OT, gt, ibt, obt, fg, Wc,
-    E, st, stall, q, qall, bsrc, bb, PP, rh, rf, C, H, Yb, R, LB, LR, T, TR, XI, XO,
+    E, st, stall, q, qall, bsrc, bb, PP, rf, C, H, Yb, R, LB, LR, T, TR, XI, XO,
     lsem, psend, precv, dsend, drecv, ssend, srecv, qsend, qrecv, fsend, frecv, bsend, brecv,
     rsend, rrecv, asend, arecv, ysend, yrecv, xsend, xrecv, zsend, zrecv, gsend, grecv,
 ):
@@ -83,8 +83,8 @@
         return (h + (2, 1, 3, 0)[v]) % 4
 
     def patch_copy(v, k):
-        place = P_.at[wave(v), l, pl.ds(w * SUB, SUB), :]
-        dev = at(y, 2 * h + (l + k // 4) % 2, ((x + k % 4) % 4) * 2 + c)
+        place = P_.at[wave(v), l if k < 5 else 1 - l, pl.ds(w * SUB, SUB), :]
+        dev = at(y, 2 * h + 1 - l, w) if k == 4 else at(y, z, ((x + k % 4) % 4) * 2 + c)
         return remote(place, place, psend.at[v, k], precv.at[v, k], dev)
 
     def partner_copy(v, k, core):
@@ -97,7 +97,7 @@
         landed(P_.at[wave(v), ls, pl.ds((2 * xs + c) * SUB, SUB), :], precv.at[v, k])
 
     for v in range(4):
-        for k in range(1, 8):
+        for k in range(1, 5):
             patch_copy(v, k).start()
         partner_copy(v, 0, c).start()
 
@@ -121,9 +121,15 @@
 
     bias_copies("start")
 
+    def pass_on(v):
+        arrived(v, 4)
+        for k in range(5, 8):
+            patch_copy(v, k).start()
+        partner_copy(v, 4, c).start()
+
     def receive(v, first, last):
         for k in range(first, last):
-            if k > 0:
+            if k not in (0, 4):
                 arrived(v, k)
                 partner_copy(v, k, c).start()
         for k in range(first, last):
@@ -138,7 +144,23 @@
         return jnp.where(l == 0, v[:, :FB], v[:, FB:])
 
     embed_bias = my_half(be)
+    gains16 = jnp.broadcast_to(gain, (16, FB))
+    gains_hi = gains16.astype(BF16)
+    gains_lo = (gains16 - gains_hi.astype(F32)).astype(BF16)
+    product = jnp.dot(gains_hi, IT[...], preferred_element_type=F32)
+    product = product + jnp.dot(gains_lo, IT[...], preferred_element_type=F32)
+    q[...] = product[0:1, :]
+
+    def q_copy(k):
+        return remote(q, qall.at[k], qsend.at[k], qrecv.at[k], at(y, (z + k) % 8, w))
+
+    for k in range(1, 8):
+        q_copy(k).start()
     lane = lax.broadcasted_iota(jnp.int32, (TB, 128), 1)
+
+    def stat_copy(k):
+        t = (z + k) % 8
+        return remote(st.at[t], stall.at[k], ssend.at[k], srecv.at[k], at(y, t, w))
 
     def first_product(k):
         t = (z + k) % 8
@@ -149,39 +171,37 @@
         n = ((e - m) * gain).astype(BF16)
         PP[t] = jnp.dot(n, IT[...], preferred_element_type=F32).astype(BF16)
         st[t] = jnp.where(lane == 0, m, jnp.where(lane == 1, s2, 0.0)).T[0:8, :]
-
-    def stat_copy(k):
-        t = (z + k) % 8
-        return remote(st.at[t], stall.at[k], ssend.at[k], srecv.at[k], at(y, t, w))
+        if not isinstance(k, int) or k > 0:
+            stat_copy(k).start()
 
     def towards(d, k):
-        return (z + k) % 8 if d == 0 else (z + 8 - k) % 8
-
-    def rows_of(d):
-        return pl.ds(d * (TB // 2), TB // 2)
+        return (z + 8 + (1 - 2 * d) * k) % 8
+
+    outward, inward = 1 - l, l
 
     def lanes_of(u):
         return pl.ds(u * HU, HU)
 
     def reduce_copy(d, s, u):
-        t = towards(d, 5 - s)
-        if s == 1:
-            src, dst = PP.at[t, rows_of(d), lanes_of(u)], rh.at[d, :, lanes_of(u)]
-        else:
-            src, dst = PP.at[t, :, lanes_of(u)], rf.at[d, s - 2, :, lanes_of(u)]
+        src = PP.at[towards(d, 5 - s), :, lanes_of(u)]
+        dst = rf.at[d, s - 1, :, lanes_of(u)]
         return remote(src, dst, rsend.at[d, s - 1, u], rrecv.at[d, s - 1, u], at(y, towards(d, 1), w))
+
+    def add_received(d, s, u):
+        landed(rf.at[d, s - 2, :, lanes_of(u)], rrecv.at[d, s - 2, u])
+        to = (towards(d, 5 - s), slice(None), lanes_of(u))
+        PP[to] = (PP[to].astype(F32) + rf[d, s - 2, :, lanes_of(u)].astype(F32)).astype(BF16)
 
     def reduce_step(s):
         for u in range(2):
-            for d in range(2):
-                reduce_copy(d, s - 1, u).wait_recv()
-                t = towards(d, 5 - s)
-                if s == 2:
-                    to, add = (t, rows_of(d), lanes_of(u)), rh[d, :, lanes_of(u)]
-                else:
-                    to, add = (t, slice(None), lanes_of(u)), rf[d, s - 3, :, lanes_of(u)]
-                PP[to] = (PP[to].astype(F32) + add.astype(F32)).astype(BF16)
-                reduce_copy(d, s, u).start()
+            if s == 2:
+                reduce_copy(outward, s, u).start()
+                add_received(inward, s, u)
+                reduce_copy(inward, s, u).start()
+            else:
+                for d in range(2):
+                    add_received(d, s, u)
+                    reduce_copy(d, s, u).start()
 
     def two_products(low, high):
         def one(n, _):
@@ -191,10 +211,12 @@
         lax.fori_loop(0, 2, one, 0)
 
     receive(0, 0, 4)
+    pass_on(0)
     first_product(4)
     for u in range(2):
-        for d in range(2):
-            reduce_copy(d, 1, u).start()
+        reduce_copy(outward, 1, u).start()
+    for v in (1, 2, 3):
+        pass_on(v)
 
     loads[8].wait()
     quarter = pl.ds(pl.multiple_of(y * QUARTER, 64), QUARTER)
@@ -270,20 +292,6 @@
     cross(1)
     first_product(0)
     for k in range(1, 8):
-        stat_copy(k).start()
-    gains16 = jnp.broadcast_to(gain, (16, FB))
-    gains_hi = gains16.astype(BF16)
-    gains_lo = (gains16 - gains_hi.astype(F32)).astype(BF16)
-    product = jnp.dot(gains_hi, IT[...], preferred_element_type=F32)
-    product = product + jnp.dot(gains_lo, IT[...], preferred_element_type=F32)
-    q[...] = product[0:1, :]
-
-    def q_copy(k):
-        return remote(q, qall.at[k], qsend.at[k], qrecv.at[k], at(y, (z + k) % 8, w))
-
-    for k in range(1, 8):
-        q_copy(k).start()
-    for k in range(1, 8):
         stat_copy(k).wait_recv()
         q_copy(k).wait_recv()
 
@@ -304,15 +312,14 @@
         landed(bb.at[u], brecv.at[u])
 
     def gather_copy(d, s, u):
-        t = towards(1 - d, s - 1)
-        ref = H.at[t, :, lanes_of(u)] if s < 4 else H.at[t, rows_of(d), lanes_of(u)]
+        ref = H.at[towards(1 - d, s - 1), :, lanes_of(u)]
         return remote(ref, ref, asend.at[d, s - 1, u], arecv.at[d, s - 1, u], at(y, towards(d, 1), w))
 
     for u in range(2):
         lanes = slice(u * HU, (u + 1) * HU)
         for d in range(2):
             reduce_copy(d, 4, u).wait_recv()
-        v = C[:, lanes] + rf[0, 2, :, lanes].astype(F32) + rf[1, 2, :, lanes].astype(F32)
+        v = C[:, lanes] + rf[0, 3, :, lanes].astype(F32) + rf[1, 3, :, lanes].astype(F32)
         v = v * cols[:, ZS:ZS + 1] + bb[u, 0:1, :]
         H[z, :, lanes_of(u)] = (0.5 * v * (1.0 + lax.erf(v * 0.7071067811865476))).astype(BF16)
         for d in range(2):
@@ -331,8 +338,11 @@
     for s in range(2, 5):
         for u in range(2):
             for d in range(2):
-                gather_copy(d, s - 1, u).wait_recv()
-                gather_copy(d, s, u).start()
+                landed(H.at[towards(1 - d, s - 1), :, lanes_of(u)], arecv.at[d, s - 2, u])
+                if s < 4:
+                    gather_copy(d, s, u).start()
+            if s == 4:
+                gather_copy(outward, s, u).start()
 
         def pair(d, _):
             second_product((z + 8 + (2 * d - 1) * (s - 1)) % 8)
@@ -355,8 +365,7 @@
         jnp.broadcast_to(final_gain, (128, FB)).T[:, 0:1] * weights.astype(F32), axis=0, keepdims=True
     )
     for u in range(2):
-        for d in range(2):
-            gather_copy(d, 4, u).wait_recv()
+        landed(H.at[(z + 4) % 8, :, lanes_of(u)], arecv.at[inward, 3, u])
     second_product((z + 4) % 8)
 
     landed(R, yrecv)
@@ -422,12 +431,27 @@
         q_copy(k).wait_send()
         for copy in last_copies(k):
             copy.wait_send()
-    for s in range(1, 5):
-        for u in range(2):
+    for u in range(2):
+        reduce_copy(outward, 1, u).wait_send()
+        gather_copy(outward, 4, u).wait_send()
+        for s in range(1, 4):
             for d in range(2):
-                reduce_copy(d, s, u).wait_send()
+                reduce_copy(d, s + 1, u).wait_send()
                 gather_copy(d, s, u).wait_send()
     landed(R, ysend)
+
+
+def write_out(new_in, new_out, logits, in_w, out_w, check, sem):
+    copies = [pltpu.make_async_copy(logits, check, sem.at[4])]
+    for n, (src, dst) in enumerate(((new_in, in_w), (new_out, out_w))):
+        rows = src.shape[0] // 2
+        for half in range(2):
+            part = pl.ds(half * rows, rows)
+            copies.append(pltpu.make_async_copy(src.at[part, :], dst.at[part, :], sem.at[2 * n + half]))
+    for copy in copies:
+        copy.start()
+    for copy in copies:
+        copy.wait()
 
 
 def on_device(
@@ -469,8 +493,7 @@
             pltpu.VMEM((8, HU), F32),
             pltpu.VMEM((2, 8, HU), F32),
             pltpu.VMEM((ZS, TB, HB), BF16),
-            pltpu.VMEM((2, TB // 2, HB), BF16),
-            pltpu.VMEM((2, 3, TB, HB), BF16),
+            pltpu.VMEM((2, 4, TB, HB), BF16),
             pltpu.VMEM((TB, HB), F32),
             pltpu.VMEM((ZS, TB, HB), BF16),
             pltpu.VMEM((ZS, TB, FB), BF16),
@@ -494,7 +517,19 @@
         *map(pinned, (patches.reshape(4, SUB, PATCH), embed_weight, embed_bias, old_in, old_out)), restore_id, *map(pinned, (
         norm_gains, in_biases, out_biases, final_gain, check_weight,
     )))
-    return new_in.reshape(2 * FB, HU), new_out, logits
+    return pl.pallas_call(
+        write_out,
+        name="write_out",
+        out_shape=(
+            jax.ShapeDtypeStruct((2 * FB, HU), BF16),
+            jax.ShapeDtypeStruct((HU, 2 * FB), BF16),
+            jax.ShapeDtypeStruct((64, CHECK), F32),
+        ),
+        in_specs=[vmem] * 3,
+        out_specs=(hbm, hbm, hbm),
+        scratch_shapes=[dma((5,))],
+        compiler_params=pltpu.CompilerParams(vmem_limit_bytes=2**20),
+    )(new_in.reshape(2 * FB, HU), new_out, logits)
 
 
 def solution(mesh):

time: 116 us -> 124 us (1.069)
  Pallas kernels: 111 us -> 122 us
  local copies, waits for them, and re-layouts: 3.43 us -> 0 us
    pallas_call x1, Pallas kernels: 111 us -> 120 us  [on_device(): pl.pallas_call(kernel, name='relayout_forward', out_shape=(jax.ShapeDtype...]
    unnamed x3 -> x0, local copies, waits for them, and re-layouts: 3.43 us -> none
    pallas_call x0 -> x1, Pallas kernels: none -> 2.23 us  [on_device(): pl.pallas_call(write_out, name='write_out', out_shape=(jax.ShapeDtypeStru...]
where the time goes in v3:
time: 124 us; the launch traced here: 123 us
  Pallas kernels  122 us (98%)
  between operations  1.29 us (1%)
    pallas_call x1, Pallas kernels, on_device(): pl.pallas_call(kernel, name='relayout_forward', out_shape=(jax.ShapeDtype...  120 us

profile of v3, /device:TPU:24, one launch (start us, length us, event | category | flops | bytes accessed | tf_op | source)
XLA Modules:
  0.0 123.1 jit_solution(1202155151479645850)
XLA Ops:
  1.3 119.5 %relayout_forward.1 = (bf16[2,768,768]{2,1,0:T(8,128)(2,1)S(1)}, bf16[768,1536]{1,0:T(8,128)(2,1)S(1)}, f32[64,128]{1,0:T(8,128)S(1)}) custom-call(bf16[4,16,588]{2,1,0:T(8,128)(2,1)} %bitcast.3, bf16[588,1536]{1,0:T(8,128)(2,1)} %embed_w.1, f32[1536]{0:T(1024)} %embed_b.1, bf16[1,768,1536]{2,1,0:T(8,128)(2,1)} %old_in.1, bf16[1,1536,768]{2,1,0:T(8,128)(2,1)} %old_out.1, ...), custom_call_target="tpu_custom_call" | custom-call | tf_op jit(solution)/shard_map/relayout_forward/pallas_call | solution.py:467
  120.8 2.2 %write_out.1 = (bf16[1536,768]{1,0:T(8,128)(2,1)}, bf16[768,1536]{1,0:T(8,128)(2,1)}, f32[64,128]{1,0:T(8,128)}) custom-call(bf16[1536,768]{1,0:T(8,128)(2,1)S(1)} %bitcast.2, bf16[768,1536]{1,0:T(8,128)(2,1)S(1)} %get-tuple-element.7.new_out, f32[64,128]{1,0:T(8,128)S(1)} %get-tuple-element.8.logits), custom_call_target="tpu_custom_call" | custom-call | tf_op jit(solution)/shard_map/write_out/pallas_call | solution.py:520

commit v4 on v3

--- a/solution.py
+++ b/solution.py
@@ -246,11 +246,10 @@
                         copy = remote(src, dst, xsend.at[a, u], xrecv.at[a, n], dev)
                         copy.start() if act == "start" else copy.wait_send()
 
-    tile_copies("start")
-
     receive(0, 4, 8)
     for v in (1, 2):
         receive(v, 0, 8)
+    tile_copies("start")
     two_products(3, 5)
     reduce_step(2)
     two_products(2, 6)
@@ -262,35 +261,39 @@
         dst = new_in.at[l, quarter, :] if a == 0 else new_out.at[quarter, half]
         return remote((XI, XO)[a], dst, zsend.at[a], zrecv.at[a], at(y, 2 * h + 1 - l, w))
 
-    def spread_copy(d, a, stage):
+    def spread_copy(d, a, p, stage):
         owner = y if stage == 0 else (y + 3 if d == 0 else y + 1) % REPS
         if stage == 0:
             rows = pl.ds(pl.multiple_of(owner * QUARTER, 64), QUARTER)
         else:
             rows = pl.ds(pl.multiple_of(owner * QUARTER + d * (QUARTER // 2), 32), QUARTER // 2)
-        ref = new_in.at[:, rows, :] if a == 0 else new_out.at[rows, :]
+        s = l if p == 0 else 1 - l
+        ref = new_in.at[s, rows, :] if a == 0 else new_out.at[rows, pl.ds(pl.multiple_of(s * FB, 128), FB)]
         to = (y + 1 if d == 0 else y + 3) % REPS
-        return remote(ref, ref, gsend.at[d, a, stage], grecv.at[d, a, stage], (to, h, col))
+        return remote(ref, ref, gsend.at[d, a, p, stage], grecv.at[d, a, p, stage], (to, h, col))
 
     def cross(a):
         landed((XI, XO)[a], xrecv.at[a, 1])
         cross_copy(a).start()
 
-    def spread(a):
-        landed(new_in.at[l, quarter, :] if a == 0 else new_out.at[quarter, half], xrecv.at[a, 0])
-        cross_copy(a).wait_recv()
+    def spread(a, p):
+        if p == 0:
+            landed(new_in.at[l, quarter, :] if a == 0 else new_out.at[quarter, half], xrecv.at[a, 0])
+        else:
+            cross_copy(a).wait_recv()
         for d in range(2):
-            spread_copy(d, a, 0).start()
-
-    def spread_on(a):
+            spread_copy(d, a, p, 0).start()
+
+    def spread_on(a, p):
         for d in range(2):
-            spread_copy(d, a, 0).wait_recv()
-            spread_copy(d, a, 1).start()
-
+            spread_copy(d, a, p, 0).wait_recv()
+            spread_copy(d, a, p, 1).start()
+
+    reduce_step(4)
     cross(0)
-    reduce_step(4)
-    cross(1)
     first_product(0)
+    spread(0, 0)
+    spread(1, 0)
     for k in range(1, 8):
         stat_copy(k).wait_recv()
         q_copy(k).wait_recv()
@@ -333,7 +336,6 @@
                 Yb.at[t, pl.ds(pl.multiple_of(to * SUB, SUB), SUB), :], R.at[k - 1, t], ysend, yrecv, at(y, z, to)
             ).start()
 
-    spread(0)
     second_product(z)
     for s in range(2, 5):
         for u in range(2):
@@ -343,6 +345,8 @@
                     gather_copy(d, s, u).start()
             if s == 4:
                 gather_copy(outward, s, u).start()
+        if s == 3:
+            cross(1)
 
         def pair(d, _):
             second_product((z + 8 + (2 * d - 1) * (s - 1)) % 8)
@@ -350,11 +354,11 @@
 
         lax.fori_loop(0, 2, pair, 0)
         if s == 2:
-            spread(1)
-        if s == 3:
-            spread_on(0)
+            spread(0, 1)
+            spread_on(0, 0)
+            spread_on(1, 0)
         if s == 4:
-            spread_on(1)
+            spread_on(0, 1)
 
     for n in (5, 6, 7):
         loads[n].wait()
@@ -368,6 +372,7 @@
         landed(H.at[(z + 4) % 8, :, lanes_of(u)], arecv.at[inward, 3, u])
     second_product((z + 4) % 8)
 
+    spread(1, 1)
     landed(R, yrecv)
     mine = pl.ds(pl.multiple_of(w * SUB, SUB), SUB)
     row = lax.broadcasted_iota(jnp.int32, (8, 128), 0)
@@ -402,6 +407,7 @@
     for k in range(1, 8):
         for copy in last_copies(k):
             copy.start()
+    spread_on(1, 1)
     for k in range(1, 8):
         for copy in last_copies(k):
             copy.wait_recv()
@@ -415,10 +421,11 @@
 
     for a in range(2):
         cross_copy(a).wait_send()
-        for d in range(2):
-            spread_copy(d, a, 1).wait_recv()
-            spread_copy(d, a, 0).wait_send()
-            spread_copy(d, a, 1).wait_send()
+        for p in range(2):
+            for d in range(2):
+                spread_copy(d, a, p, 1).wait_recv()
+                spread_copy(d, a, p, 0).wait_send()
+                spread_copy(d, a, p, 1).wait_send()
     tile_copies("wait")
     bias_copies("wait")
     for v in range(4):
@@ -508,7 +515,7 @@
             dma((8,)), dma((8,)), dma((8,)), dma((8,)), dma((2, 8)), dma((2, 8)), dma((2,)), dma((2,)),
             dma((2, 4, 2)), dma((2, 4, 2)), dma((2, 4, 2)), dma((2, 4, 2)),
             dma, dma,
-            dma((2, 2)), dma((2, 2)), dma((2,)), dma((2,)), dma((2, 2, 2)), dma((2, 2, 2)),
+            dma((2, 2)), dma((2, 2)), dma((2,)), dma((2,)), dma((2, 2, 2, 2)), dma((2, 2, 2, 2)),
         ],
         compiler_params=pltpu.CompilerParams(
             collective_id=0, has_side_effects=True, vmem_limit_bytes=36 * 2**20

time: 124 us -> 108 us (0.87)
  Pallas kernels: 122 us -> 106 us
    pallas_call x1, Pallas kernels: 120 us -> 104 us  [on_device(): pl.pallas_call(kernel, name='relayout_forward', out_shape=(jax.ShapeDtype...]
where the time goes in v4:
time: 108 us
  Pallas kernels  106 us (98%)
  between operations  1.29 us (1%)
    pallas_call x1, Pallas kernels, on_device(): pl.pallas_call(kernel, name='relayout_forward', out_shape=(jax.ShapeDtype...  104 us
    pallas_call x1, Pallas kernels, on_device(): pl.pallas_call(write_out, name='write_out', out_shape=(jax.ShapeDtypeStru...  2.23 us

profile of v4, /device:TPU:24, one launch (start us, length us, event | category | flops | bytes accessed | tf_op | source)
XLA Modules:
  0.0 107.7 jit_solution(15907918815212223477)
XLA Ops:
  1.3 104.2 %relayout_forward.1 = (bf16[2,768,768]{2,1,0:T(8,128)(2,1)S(1)}, bf16[768,1536]{1,0:T(8,128)(2,1)S(1)}, f32[64,128]{1,0:T(8,128)S(1)}) custom-call(bf16[4,16,588]{2,1,0:T(8,128)(2,1)} %bitcast.3, bf16[588,1536]{1,0:T(8,128)(2,1)} %embed_w.1, f32[1536]{0:T(1024)} %embed_b.1, bf16[1,768,1536]{2,1,0:T(8,128)(2,1)} %old_in.1, bf16[1,1536,768]{2,1,0:T(8,128)(2,1)} %old_out.1, ...), custom_call_target="tpu_custom_call" | custom-call | tf_op jit(solution)/shard_map/relayout_forward/pallas_call | solution.py:474
  105.4 2.2 %write_out.1 = (bf16[1536,768]{1,0:T(8,128)(2,1)}, bf16[768,1536]{1,0:T(8,128)(2,1)}, f32[64,128]{1,0:T(8,128)}) custom-call(bf16[1536,768]{1,0:T(8,128)(2,1)S(1)} %bitcast.2, bf16[768,1536]{1,0:T(8,128)(2,1)S(1)} %get-tuple-element.7.new_out, f32[64,128]{1,0:T(8,128)S(1)} %get-tuple-element.8.logits), custom_call_target="tpu_custom_call" | custom-call | tf_op jit(solution)/shard_map/write_out/pallas_call | solution.py:527

commit v5 on v3

--- a/solution.py
+++ b/solution.py
@@ -29,7 +29,7 @@
     P_, We, be, IT, OT, gt, ibt, obt, fg, Wc,
     E, st, stall, q, qall, bsrc, bb, PP, rf, C, H, Yb, R, LB, LR, T, TR, XI, XO,
     lsem, psend, precv, dsend, drecv, ssend, srecv, qsend, qrecv, fsend, frecv, bsend, brecv,
-    rsend, rrecv, asend, arecv, ysend, yrecv, xsend, xrecv, zsend, zrecv, gsend, grecv,
+    rsend, rrecv, asend, arecv, ysend, yrecv, xsend, xrecv, zsend, zrecv, gsend, grecv, gend,
 ):
     y, h, col = lax.axis_index("rep"), lax.axis_index("row"), lax.axis_index("col")
     l, w = col // 8, col % 8
@@ -79,27 +79,31 @@
 
     partner = at(y, z, 2 * x + 1 - c)
 
-    def wave(v):
-        return (h + (2, 1, 3, 0)[v]) % 4
+    def wave(v, plane):
+        return (h + 2 + (v % 2) * (1 - 2 * plane)) % 4 if v < 2 else (h + (1 + 2 * plane if v == 2 else 0)) % 4
 
     def patch_copy(v, k):
-        place = P_.at[wave(v), l if k < 5 else 1 - l, pl.ds(w * SUB, SUB), :]
+        plane = l if k < 5 else 1 - l
+        place = P_.at[wave(v, plane), plane, pl.ds(w * SUB, SUB), :]
         dev = at(y, 2 * h + 1 - l, w) if k == 4 else at(y, z, ((x + k % 4) % 4) * 2 + c)
-        return remote(place, place, psend.at[v, k], precv.at[v, k], dev)
+        return remote(place, place, psend, precv.at[v, 0 if k < 4 else 1 if k == 4 else 2], dev)
 
     def partner_copy(v, k, core):
         ls, xs = (l + k // 4) % 2, (x + 4 - k % 4) % 4
-        piece = P_.at[wave(v), ls, pl.ds((2 * xs + core) * SUB, SUB), :]
-        return remote(piece, piece, dsend.at[v, k], drecv.at[v, k], partner)
-
-    def arrived(v, k):
-        ls, xs = (l + k // 4) % 2, (x + 4 - k % 4) % 4
-        landed(P_.at[wave(v), ls, pl.ds((2 * xs + c) * SUB, SUB), :], precv.at[v, k])
+        piece = P_.at[wave(v, ls), ls, pl.ds((2 * xs + core) * SUB, SUB), :]
+        if v == 0 and k < 4 and core is c:
+            piece = P_.at[wave(v, l), l, pl.ds(w * SUB, SUB), :]
+            return remote(piece, piece, dsend, drecv.at[v, 0], at(y, z, ((x + k) % 4) * 2 + 1 - c))
+        return remote(piece, piece, dsend, drecv.at[v, k // 4 if v == 0 else 0], partner)
+
+    def arrived(n, sem):
+        landed(P_.at[0, 0, pl.ds(0, n * SUB), :], sem)
 
     for v in range(4):
         for k in range(1, 5):
             patch_copy(v, k).start()
-        partner_copy(v, 0, c).start()
+        for k in range(4 if v == 0 else 1):
+            partner_copy(v, k, c).start()
 
     loads[3].wait()
     bsrc[...] = jnp.broadcast_to(ibt[pl.ds(rid[0], 1), :], bsrc.shape)
@@ -122,18 +126,22 @@
     bias_copies("start")
 
     def pass_on(v):
-        arrived(v, 4)
+        arrived(1, precv.at[v, 1])
         for k in range(5, 8):
             patch_copy(v, k).start()
         partner_copy(v, 4, c).start()
 
     def receive(v, first, last):
-        for k in range(first, last):
-            if k not in (0, 4):
-                arrived(v, k)
+        if first == 0:
+            arrived(3, precv.at[v, 0])
+            for k in range(1, 4):
+                if v > 0:
+                    partner_copy(v, k, c).start()
+        if last == 8:
+            arrived(3, precv.at[v, 2])
+            for k in range(5, 8):
                 partner_copy(v, k, c).start()
-        for k in range(first, last):
-            partner_copy(v, k, 1 - c).wait_recv()
+        arrived(last - first, drecv.at[v, first // 4])
 
     for n in (0, 1, 2, 4):
         loads[n].wait()
@@ -152,7 +160,7 @@
     q[...] = product[0:1, :]
 
     def q_copy(k):
-        return remote(q, qall.at[k], qsend.at[k], qrecv.at[k], at(y, (z + k) % 8, w))
+        return remote(q, qall.at[k], qsend, qrecv, at(y, (z + k) % 8, w))
 
     for k in range(1, 8):
         q_copy(k).start()
@@ -160,7 +168,7 @@
 
     def stat_copy(k):
         t = (z + k) % 8
-        return remote(st.at[t], stall.at[k], ssend.at[k], srecv.at[k], at(y, t, w))
+        return remote(st.at[t], stall.at[k], ssend, srecv, at(y, t, w))
 
     def first_product(k):
         t = (z + k) % 8
@@ -177,31 +185,29 @@
     def towards(d, k):
         return (z + 8 + (1 - 2 * d) * k) % 8
 
-    outward, inward = 1 - l, l
 
     def lanes_of(u):
         return pl.ds(u * HU, HU)
 
+    def rows_of(d, s):
+        return pl.ds(d * (TB // 2), TB // 2) if s == 1 else slice(None)
+
     def reduce_copy(d, s, u):
-        src = PP.at[towards(d, 5 - s), :, lanes_of(u)]
-        dst = rf.at[d, s - 1, :, lanes_of(u)]
-        return remote(src, dst, rsend.at[d, s - 1, u], rrecv.at[d, s - 1, u], at(y, towards(d, 1), w))
+        src = PP.at[towards(d, 5 - s), rows_of(d, s), lanes_of(u)]
+        dst = rf.at[d, s - 1, rows_of(d, s), lanes_of(u)]
+        return remote(src, dst, rsend, rrecv.at[d, s - 1, u], at(y, towards(d, 1), w))
 
     def add_received(d, s, u):
-        landed(rf.at[d, s - 2, :, lanes_of(u)], rrecv.at[d, s - 2, u])
-        to = (towards(d, 5 - s), slice(None), lanes_of(u))
-        PP[to] = (PP[to].astype(F32) + rf[d, s - 2, :, lanes_of(u)].astype(F32)).astype(BF16)
+        rows = rows_of(d, s - 1)
+        landed(rf.at[d, s - 2, rows, lanes_of(u)], rrecv.at[d, s - 2, u])
+        to = (towards(d, 5 - s), rows, lanes_of(u))
+        PP[to] = (PP[to].astype(F32) + rf[d, s - 2, rows, lanes_of(u)].astype(F32)).astype(BF16)
 
     def reduce_step(s):
         for u in range(2):
-            if s == 2:
-                reduce_copy(outward, s, u).start()
-                add_received(inward, s, u)
-                reduce_copy(inward, s, u).start()
-            else:
-                for d in range(2):
-                    add_received(d, s, u)
-                    reduce_copy(d, s, u).start()
+            for d in range(2):
+                add_received(d, s, u)
+                reduce_copy(d, s, u).start()
 
     def two_products(low, high):
         def one(n, _):
@@ -214,7 +220,8 @@
     pass_on(0)
     first_product(4)
     for u in range(2):
-        reduce_copy(outward, 1, u).start()
+        for d in range(2):
+            reduce_copy(d, 1, u).start()
     for v in (1, 2, 3):
         pass_on(v)
 
@@ -246,54 +253,59 @@
                         copy = remote(src, dst, xsend.at[a, u], xrecv.at[a, n], dev)
                         copy.start() if act == "start" else copy.wait_send()
 
+    receive(0, 4, 8)
+    first_product(5 - 2 * l)
+    receive(1, 0, 8)
+    first_product(3 + 2 * l)
+    reduce_step(2)
+    receive(2, 0, 8)
     tile_copies("start")
-
-    receive(0, 4, 8)
-    for v in (1, 2):
-        receive(v, 0, 8)
-    two_products(3, 5)
-    reduce_step(2)
     two_products(2, 6)
     receive(3, 0, 8)
     reduce_step(3)
     two_products(1, 7)
 
-    def cross_copy(a):
-        dst = new_in.at[l, quarter, :] if a == 0 else new_out.at[quarter, half]
-        return remote((XI, XO)[a], dst, zsend.at[a], zrecv.at[a], at(y, 2 * h + 1 - l, w))
-
-    def spread_copy(d, a, stage):
+    pieces = ((0, 0, 0, QUARTER), (1, 0, 0, QUARTER), (0, 1, 0, QUARTER), (1, 1, 0, QUARTER // 2), (1, 1, QUARTER // 2, QUARTER // 2))
+
+    def piece_ref(i, plane, owner, skip, n):
+        rows = pl.ds(pl.multiple_of(owner * QUARTER + pieces[i][2] + skip, 16), n)
+        if pieces[i][0] == 0:
+            return new_in.at[plane, rows, :]
+        return new_out.at[rows, pl.ds(pl.multiple_of(plane * FB, 128), FB)]
+
+    def cross_copy(i):
+        n = pieces[i][3]
+        src = (XI, XO)[pieces[i][0]].at[pl.ds(pieces[i][2], n), :]
+        return remote(src, piece_ref(i, l, y, 0, n), zsend.at[i - 2], zrecv.at[i - 2], at(y, 2 * h + 1 - l, w))
+
+    def spread_copy(d, i, stage):
         owner = y if stage == 0 else (y + 3 if d == 0 else y + 1) % REPS
-        if stage == 0:
-            rows = pl.ds(pl.multiple_of(owner * QUARTER, 64), QUARTER)
+        n = pieces[i][3] if stage == 0 else pieces[i][3] // 2
+        ref = piece_ref(i, 1 - l if pieces[i][1] else l, owner, 0 if stage == 0 else d * n, n)
+        to = (y + 1 if d == 0 else y + 3) % REPS
+        return remote(ref, ref, gsend.at[d], grecv.at[d, i] if stage == 0 else gend, (to, h, col))
+
+    def spread(i):
+        if pieces[i][1]:
+            cross_copy(i).wait_recv()
         else:
-            rows = pl.ds(pl.multiple_of(owner * QUARTER + d * (QUARTER // 2), 32), QUARTER // 2)
-        ref = new_in.at[:, rows, :] if a == 0 else new_out.at[rows, :]
-        to = (y + 1 if d == 0 else y + 3) % REPS
-        return remote(ref, ref, gsend.at[d, a, stage], grecv.at[d, a, stage], (to, h, col))
-
-    def cross(a):
-        landed((XI, XO)[a], xrecv.at[a, 1])
-        cross_copy(a).start()
-
-    def spread(a):
-        landed(new_in.at[l, quarter, :] if a == 0 else new_out.at[quarter, half], xrecv.at[a, 0])
-        cross_copy(a).wait_recv()
+            landed(piece_ref(i, l, y, 0, QUARTER), xrecv.at[pieces[i][0], 0])
         for d in range(2):
-            spread_copy(d, a, 0).start()
-
-    def spread_on(a):
+            spread_copy(d, i, 0).start()
+
+    def spread_on(i):
         for d in range(2):
-            spread_copy(d, a, 0).wait_recv()
-            spread_copy(d, a, 1).start()
-
-    cross(0)
+            spread_copy(d, i, 0).wait_recv()
+            spread_copy(d, i, 1).start()
+
     reduce_step(4)
-    cross(1)
+    landed(XI, xrecv.at[0, 1])
+    cross_copy(2).start()
     first_product(0)
-    for k in range(1, 8):
-        stat_copy(k).wait_recv()
-        q_copy(k).wait_recv()
+    spread(0)
+    spread(1)
+    landed(stall.at[pl.ds(1, 7)], srecv)
+    landed(qall.at[pl.ds(1, 7)], qrecv)
 
     def columns_of(tiles):
         mean = functools.reduce(jnp.add, [t[0:1] for t in tiles]) / ZS
@@ -311,9 +323,11 @@
         C[:, lanes] = v
         landed(bb.at[u], brecv.at[u])
 
+    outward, inward = 1 - l, l
+
     def gather_copy(d, s, u):
         ref = H.at[towards(1 - d, s - 1), :, lanes_of(u)]
-        return remote(ref, ref, asend.at[d, s - 1, u], arecv.at[d, s - 1, u], at(y, towards(d, 1), w))
+        return remote(ref, ref, asend, arecv.at[d, s - 1, u], at(y, towards(d, 1), w))
 
     for u in range(2):
         lanes = slice(u * HU, (u + 1) * HU)
@@ -333,7 +347,6 @@
                 Yb.at[t, pl.ds(pl.multiple_of(to * SUB, SUB), SUB), :], R.at[k - 1, t], ysend, yrecv, at(y, z, to)
             ).start()
 
-    spread(0)
     second_product(z)
     for s in range(2, 5):
         for u in range(2):
@@ -343,6 +356,10 @@
                     gather_copy(d, s, u).start()
             if s == 4:
                 gather_copy(outward, s, u).start()
+        if s == 3:
+            landed(XO, xrecv.at[1, 1])
+            cross_copy(3).start()
+            cross_copy(4).start()
 
         def pair(d, _):
             second_product((z + 8 + (2 * d - 1) * (s - 1)) % 8)
@@ -350,11 +367,12 @@
 
         lax.fori_loop(0, 2, pair, 0)
         if s == 2:
-            spread(1)
-        if s == 3:
+            spread(2)
             spread_on(0)
+            spread_on(1)
         if s == 4:
-            spread_on(1)
+            spread_on(2)
+            spread(3)
 
     for n in (5, 6, 7):
         loads[n].wait()
@@ -368,7 +386,9 @@
         landed(H.at[(z + 4) % 8, :, lanes_of(u)], arecv.at[inward, 3, u])
     second_product((z + 4) % 8)
 
+    spread(4)
     landed(R, yrecv)
+    spread_on(3)
     mine = pl.ds(pl.multiple_of(w * SUB, SUB), SUB)
     row = lax.broadcasted_iota(jnp.int32, (8, 128), 0)
     columns = []
@@ -395,16 +415,16 @@
     def last_copies(k):
         dev = at(y, (z + k) % 8, w)
         return (
-            remote(LB.at[(z + k) % 2], LR.at[k - 1], fsend.at[0, k], frecv.at[0, k], dev),
-            remote(T, TR.at[k - 1], fsend.at[1, k], frecv.at[1, k], dev),
+            remote(LB.at[(z + k) % 2], LR.at[k - 1], fsend.at[0], frecv.at[0], dev),
+            remote(T, TR.at[k - 1], fsend.at[1], frecv.at[1], dev),
         )
 
     for k in range(1, 8):
         for copy in last_copies(k):
             copy.start()
-    for k in range(1, 8):
-        for copy in last_copies(k):
-            copy.wait_recv()
+    spread_on(4)
+    landed(LR, frecv.at[0])
+    landed(TR, frecv.at[1])
     tiles = [T[...]] + [TR[k] for k in range(7)]
     E[0, :, 0:128] = columns_of(tiles)
     cols = E[0, pl.ds(pl.multiple_of(l * 64, 64), 64), 0:128]
@@ -413,31 +433,21 @@
         v = v + LR[k].astype(F32) + cols[:, k + 1:k + 2] * tiles[k + 1][2:3]
     logits[...] = v * cols[:, ZS:ZS + 1]
 
-    for a in range(2):
-        cross_copy(a).wait_send()
-        for d in range(2):
-            spread_copy(d, a, 1).wait_recv()
-            spread_copy(d, a, 0).wait_send()
-            spread_copy(d, a, 1).wait_send()
+    landed(OT.at[pl.ds(0, 2 * FB // 2), :], gend)
+    for d in range(2):
+        landed(OT.at[pl.ds(0, HB * 3 // 4), :], gsend.at[d])
+    for i in range(2, 5):
+        cross_copy(i).wait_send()
     tile_copies("wait")
     bias_copies("wait")
-    for v in range(4):
-        for k in range(8):
-            if k > 0:
-                patch_copy(v, k).wait_send()
-            partner_copy(v, k, c).wait_send()
-    for k in range(1, 8):
-        stat_copy(k).wait_send()
-        q_copy(k).wait_send()
-        for copy in last_copies(k):
-            copy.wait_send()
-    for u in range(2):
-        reduce_copy(outward, 1, u).wait_send()
-        gather_copy(outward, 4, u).wait_send()
-        for s in range(1, 4):
-            for d in range(2):
-                reduce_copy(d, s + 1, u).wait_send()
-                gather_copy(d, s, u).wait_send()
+    landed(P_.at[:, 0, pl.ds(0, 7 * SUB), :], psend)
+    landed(P_.at[:, 0], dsend)
+    landed(stall.at[pl.ds(1, 7)], ssend)
+    landed(qall.at[pl.ds(1, 7)], qsend)
+    landed(LR, fsend.at[0])
+    landed(TR, fsend.at[1])
+    landed(PP.at[pl.ds(0, 7)], rsend)
+    landed(H.at[pl.ds(0, 7)], asend)
     landed(R, ysend)
 
 
@@ -504,11 +514,11 @@
             pltpu.VMEM((7, 8, 128), F32),
             pltpu.VMEM((QUARTER, HU), BF16),
             pltpu.VMEM((QUARTER, FB), BF16),
-            dma((10,)), dma((4, 8)), dma((4, 8)), dma((4, 8)), dma((4, 8)),
-            dma((8,)), dma((8,)), dma((8,)), dma((8,)), dma((2, 8)), dma((2, 8)), dma((2,)), dma((2,)),
-            dma((2, 4, 2)), dma((2, 4, 2)), dma((2, 4, 2)), dma((2, 4, 2)),
+            dma((10,)), dma, dma((4, 3)), dma, dma((4, 2)),
+            dma, dma, dma, dma, dma((2,)), dma((2,)), dma((2,)), dma((2,)),
+            dma, dma((2, 4, 2)), dma, dma((2, 4, 2)),
             dma, dma,
-            dma((2, 2)), dma((2, 2)), dma((2,)), dma((2,)), dma((2, 2, 2)), dma((2, 2, 2)),
+            dma((2, 2)), dma((2, 2)), dma((3,)), dma((3,)), dma((2,)), dma((2, 5)), dma,
         ],
         compiler_params=pltpu.CompilerParams(
             collective_id=0, has_side_effects=True, vmem_limit_bytes=36 * 2**20

time: 124 us -> 105 us (0.85)
  Pallas kernels: 122 us -> 103 us
    pallas_call x1, Pallas kernels: 120 us -> 101 us  [on_device(): pl.pallas_call(kernel, name='relayout_forward', out_shape=(jax.ShapeDtype...]
where the time goes in v5:
time: 105 us; the launch traced here: 104 us
  Pallas kernels  103 us (98%)
  between operations  1.29 us (1%)
    pallas_call x1, Pallas kernels, on_device(): pl.pallas_call(kernel, name='relayout_forward', out_shape=(jax.ShapeDtype...  101 us
    pallas_call x1, Pallas kernels, on_device(): pl.pallas_call(write_out, name='write_out', out_shape=(jax.ShapeDtypeStru...  2.23 us

profile of v5, /device:TPU:24, one launch (start us, length us, event | category | flops | bytes accessed | tf_op | source)
XLA Modules:
  0.0 104.4 jit_solution(16523610421358237729)
XLA Ops:
  1.3 100.9 %relayout_forward.1 = (bf16[2,768,768]{2,1,0:T(8,128)(2,1)S(1)}, bf16[768,1536]{1,0:T(8,128)(2,1)S(1)}, f32[64,128]{1,0:T(8,128)S(1)}) custom-call(bf16[4,16,588]{2,1,0:T(8,128)(2,1)} %bitcast.3, bf16[588,1536]{1,0:T(8,128)(2,1)} %embed_w.1, f32[1536]{0:T(1024)} %embed_b.1, bf16[1,768,1536]{2,1,0:T(8,128)(2,1)} %old_in.1, bf16[1,1536,768]{2,1,0:T(8,128)(2,1)} %old_out.1, ...), custom_call_target="tpu_custom_call" | custom-call | tf_op jit(solution)/shard_map/relayout_forward/pallas_call | solution.py:477
  102.2 2.2 %write_out.1 = (bf16[1536,768]{1,0:T(8,128)(2,1)}, bf16[768,1536]{1,0:T(8,128)(2,1)}, f32[64,128]{1,0:T(8,128)}) custom-call(bf16[1536,768]{1,0:T(8,128)(2,1)S(1)} %bitcast.2, bf16[768,1536]{1,0:T(8,128)(2,1)S(1)} %get-tuple-element.7.new_out, f32[64,128]{1,0:T(8,128)S(1)} %get-tuple-element.8.logits), custom_call_target="tpu_custom_call" | custom-call | tf_op jit(solution)/shard_map/write_out/pallas_call | solution.py:530

commit v6 on v5

--- a/solution.py
+++ b/solution.py
@@ -21,13 +21,15 @@
 TB = 128
 SUB = TB // WS
 QUARTER = FB // REPS
+CHUNKS = 4
+CHUNK = TB // CHUNKS
 
 
 def kernel(
     patches, embed_w, embed_b, old_in, old_out, rid, gains, in_b, out_b, final_g, check_w,
     new_in, new_out, logits,
     P_, We, be, IT, OT, gt, ibt, obt, fg, Wc,
-    E, st, stall, q, qall, bsrc, bb, PP, rf, C, H, Yb, R, LB, LR, T, TR, XI, XO,
+    E, st, stall, qown, qall, bsrc, bb, PP, rf, C, H, Yb, R, LB, LR, T, TR, XI, XO,
     lsem, psend, precv, dsend, drecv, ssend, srecv, qsend, qrecv, fsend, frecv, bsend, brecv,
     rsend, rrecv, asend, arecv, ysend, yrecv, xsend, xrecv, zsend, zrecv, gsend, grecv, gend,
 ):
@@ -35,6 +37,7 @@
     l, w = col // 8, col % 8
     x, c = w // 2, w % 2
     z = 2 * h + l
+    slot = pl.ds(pl.multiple_of((4 * c + x) * SUB, SUB), SUB)
 
     def at(yy, zz, ww):
         return (yy, zz // 2, (zz % 2) * 8 + ww)
@@ -62,7 +65,7 @@
             (old_out.at[0], OT),
         ])
     ]
-    own = pltpu.make_async_copy(patches, P_.at[:, l, pl.ds(w * SUB, SUB), :], lsem.at[9])
+    own = pltpu.make_async_copy(patches, P_.at[:, l, slot, :], lsem.at[9])
     own.start()
     for load in loads:
         load.start()
@@ -84,26 +87,30 @@
 
     def patch_copy(v, k):
         plane = l if k < 5 else 1 - l
-        place = P_.at[wave(v, plane), plane, pl.ds(w * SUB, SUB), :]
+        place = P_.at[wave(v, plane), plane, slot, :]
         dev = at(y, 2 * h + 1 - l, w) if k == 4 else at(y, z, ((x + k % 4) % 4) * 2 + c)
         return remote(place, place, psend, precv.at[v, 0 if k < 4 else 1 if k == 4 else 2], dev)
 
     def partner_copy(v, k, core):
         ls, xs = (l + k // 4) % 2, (x + 4 - k % 4) % 4
-        piece = P_.at[wave(v, ls), ls, pl.ds((2 * xs + core) * SUB, SUB), :]
+        piece = P_.at[wave(v, ls), ls, pl.ds((4 * core + xs) * SUB, SUB), :]
         if v == 0 and k < 4 and core is c:
-            piece = P_.at[wave(v, l), l, pl.ds(w * SUB, SUB), :]
+            piece = P_.at[wave(v, l), l, slot, :]
             return remote(piece, piece, dsend, drecv.at[v, 0], at(y, z, ((x + k) % 4) * 2 + 1 - c))
-        return remote(piece, piece, dsend, drecv.at[v, k // 4 if v == 0 else 0], partner)
+        return remote(piece, piece, dsend, drecv.at[v, k // 4], partner)
 
     def arrived(n, sem):
         landed(P_.at[0, 0, pl.ds(0, n * SUB), :], sem)
 
-    for v in range(4):
-        for k in range(1, 5):
+    def send_own(v):
+        for k in range(1, 4):
             patch_copy(v, k).start()
         for k in range(4 if v == 0 else 1):
             partner_copy(v, k, c).start()
+
+    send_own(0)
+    for v in range(4):
+        patch_copy(v, 4).start()
 
     loads[3].wait()
     bsrc[...] = jnp.broadcast_to(ibt[pl.ds(rid[0], 1), :], bsrc.shape)
@@ -131,17 +138,14 @@
             patch_copy(v, k).start()
         partner_copy(v, 4, c).start()
 
-    def receive(v, first, last):
-        if first == 0:
-            arrived(3, precv.at[v, 0])
-            for k in range(1, 4):
-                if v > 0:
-                    partner_copy(v, k, c).start()
-        if last == 8:
-            arrived(3, precv.at[v, 2])
-            for k in range(5, 8):
+    def share(v, plane):
+        arrived(3, precv.at[v, 2 * plane])
+        for k in range(4 * plane + 1, 4 * plane + 4):
+            if v > 0 or plane > 0:
                 partner_copy(v, k, c).start()
-        arrived(last - first, drecv.at[v, first // 4])
+
+    def complete(v, plane):
+        arrived(4, drecv.at[v, plane])
 
     for n in (0, 1, 2, 4):
         loads[n].wait()
@@ -157,10 +161,10 @@
     gains_lo = (gains16 - gains_hi.astype(F32)).astype(BF16)
     product = jnp.dot(gains_hi, IT[...], preferred_element_type=F32)
     product = product + jnp.dot(gains_lo, IT[...], preferred_element_type=F32)
-    q[...] = product[0:1, :]
+    qown[...] = product[0:1, :]
 
     def q_copy(k):
-        return remote(q, qall.at[k], qsend, qrecv, at(y, (z + k) % 8, w))
+        return remote(qown, qall.at[k], qsend, qrecv, at(y, (z + k) % 8, w))
 
     for k in range(1, 8):
         q_copy(k).start()
@@ -189,25 +193,24 @@
     def lanes_of(u):
         return pl.ds(u * HU, HU)
 
-    def rows_of(d, s):
-        return pl.ds(d * (TB // 2), TB // 2) if s == 1 else slice(None)
-
-    def reduce_copy(d, s, u):
-        src = PP.at[towards(d, 5 - s), rows_of(d, s), lanes_of(u)]
-        dst = rf.at[d, s - 1, rows_of(d, s), lanes_of(u)]
-        return remote(src, dst, rsend, rrecv.at[d, s - 1, u], at(y, towards(d, 1), w))
-
-    def add_received(d, s, u):
-        rows = rows_of(d, s - 1)
-        landed(rf.at[d, s - 2, rows, lanes_of(u)], rrecv.at[d, s - 2, u])
-        to = (towards(d, 5 - s), rows, lanes_of(u))
-        PP[to] = (PP[to].astype(F32) + rf[d, s - 2, rows, lanes_of(u)].astype(F32)).astype(BF16)
+    def rows_of(u):
+        return pl.ds(u * (TB // 2), TB // 2)
+
+    def chunk(q):
+        return pl.ds(q * CHUNK, CHUNK)
+
+    def reduce_copy(d, s, q):
+        src = PP.at[towards(d, 5 - s), chunk(q), :]
+        return remote(src, rf.at[d, s - 1, chunk(q), :], rsend, rrecv.at[d, s - 1, q], at(y, towards(d, 1), w))
 
     def reduce_step(s):
-        for u in range(2):
+        for q in range(CHUNKS):
             for d in range(2):
-                add_received(d, s, u)
-                reduce_copy(d, s, u).start()
+                if s > 2 or q * 2 // CHUNKS == d:
+                    landed(rf.at[d, s - 2, chunk(q), :], rrecv.at[d, s - 2, q])
+                    to = (towards(d, 5 - s), chunk(q), slice(None))
+                    PP[to] = (PP[to].astype(F32) + rf[d, s - 2, chunk(q), :].astype(F32)).astype(BF16)
+                reduce_copy(d, s, q).start()
 
     def two_products(low, high):
         def one(n, _):
@@ -216,14 +219,19 @@
 
         lax.fori_loop(0, 2, one, 0)
 
-    receive(0, 0, 4)
     pass_on(0)
+    pass_on(1)
+    send_own(1)
+    send_own(2)
+    share(0, 0)
+    complete(0, 0)
     first_product(4)
-    for u in range(2):
+    for q in range(CHUNKS // 2):
         for d in range(2):
-            reduce_copy(d, 1, u).start()
-    for v in (1, 2, 3):
-        pass_on(v)
+            reduce_copy(d, 1, d * CHUNKS // 2 + q).start()
+    pass_on(2)
+    pass_on(3)
+    send_own(3)
 
     loads[8].wait()
     quarter = pl.ds(pl.multiple_of(y * QUARTER, 64), QUARTER)
@@ -253,16 +261,26 @@
                         copy = remote(src, dst, xsend.at[a, u], xrecv.at[a, n], dev)
                         copy.start() if act == "start" else copy.wait_send()
 
-    receive(0, 4, 8)
+    share(0, 1)
+    complete(0, 1)
     first_product(5 - 2 * l)
-    receive(1, 0, 8)
+    share(1, 1)
+    complete(1, 1)
     first_product(3 + 2 * l)
+    share(1, 0)
+    share(2, 0)
     reduce_step(2)
-    receive(2, 0, 8)
+    complete(1, 0)
+    complete(2, 0)
+    two_products(2, 6)
+    share(2, 1)
+    share(3, 0)
+    share(3, 1)
     tile_copies("start")
-    two_products(2, 6)
-    receive(3, 0, 8)
     reduce_step(3)
+    complete(2, 1)
+    complete(3, 0)
+    complete(3, 1)
     two_products(1, 7)
 
     pieces = ((0, 0, 0, QUARTER), (1, 0, 0, QUARTER), (0, 1, 0, QUARTER), (1, 1, 0, QUARTER // 2), (1, 1, QUARTER // 2, QUARTER // 2))
@@ -315,64 +333,70 @@
         return jnp.concatenate(rows, axis=0).T
 
     cols = columns_of([st[z]] + [stall[k] for k in range(1, 8)])
+    v = PP[z].astype(F32) + cols[:, 0:1] * qown[...]
+    for k in range(1, 8):
+        v = v + cols[:, k:k + 1] * qall[k]
+    C[...] = v
     for u in range(2):
-        lanes = slice(u * HU, (u + 1) * HU)
-        v = PP[z, :, lanes_of(u)].astype(F32) + cols[:, 0:1] * q[:, lanes]
-        for k in range(1, 8):
-            v = v + cols[:, k:k + 1] * qall[k, :, lanes]
-        C[:, lanes] = v
         landed(bb.at[u], brecv.at[u])
+    in_bias = jnp.concatenate([bb[0, 0:1, :], bb[1, 0:1, :]], axis=1)
 
     outward, inward = 1 - l, l
 
-    def gather_copy(d, s, u):
-        ref = H.at[towards(1 - d, s - 1), :, lanes_of(u)]
-        return remote(ref, ref, asend, arecv.at[d, s - 1, u], at(y, towards(d, 1), w))
+    def gather_copy(d, s, q):
+        ref = H.at[towards(1 - d, s - 1), chunk(q), :]
+        return remote(ref, ref, asend, arecv.at[d, s - 1, q], at(y, towards(d, 1), w))
+
+    for q in range(CHUNKS):
+        rows = slice(q * CHUNK, (q + 1) * CHUNK)
+        for d in range(2):
+            reduce_copy(d, 4, q).wait_recv()
+        v = C[rows, :] + rf[0, 3, rows, :].astype(F32) + rf[1, 3, rows, :].astype(F32)
+        v = v * cols[rows, ZS:ZS + 1] + in_bias
+        H[z, rows, :] = (0.5 * v * (1.0 + lax.erf(v * 0.7071067811865476))).astype(BF16)
+        for d in range(2):
+            gather_copy(d, 1, q).start()
+
+    def second_product(t, u):
+        Yb[t, rows_of(u), :] = jnp.dot(H[t, rows_of(u), :], OT[...], preferred_element_type=F32).astype(BF16)
+        for k in range(4):
+            to = (x + k) % 4
+            copy = remote(
+                Yb.at[t, pl.ds(pl.multiple_of((4 * u + to) * SUB, SUB), SUB), :], R.at[(2 * k + u - c + 8) % 8 - 1, t],
+                ysend, yrecv, at(y, z, 2 * to + u),
+            )
+            if k > 0:
+                copy.start()
+            else:
+                pl.when(c != u)(copy.start)
 
     for u in range(2):
-        lanes = slice(u * HU, (u + 1) * HU)
-        for d in range(2):
-            reduce_copy(d, 4, u).wait_recv()
-        v = C[:, lanes] + rf[0, 3, :, lanes].astype(F32) + rf[1, 3, :, lanes].astype(F32)
-        v = v * cols[:, ZS:ZS + 1] + bb[u, 0:1, :]
-        H[z, :, lanes_of(u)] = (0.5 * v * (1.0 + lax.erf(v * 0.7071067811865476))).astype(BF16)
-        for d in range(2):
-            gather_copy(d, 1, u).start()
-
-    def second_product(t):
-        Yb[t] = jnp.dot(H[t], OT[...], preferred_element_type=F32).astype(BF16)
-        for k in range(1, 8):
-            to = (w + k) % 8
-            remote(
-                Yb.at[t, pl.ds(pl.multiple_of(to * SUB, SUB), SUB), :], R.at[k - 1, t], ysend, yrecv, at(y, z, to)
-            ).start()
-
-    second_product(z)
+        second_product(z, u)
     for s in range(2, 5):
         for u in range(2):
-            for d in range(2):
-                landed(H.at[towards(1 - d, s - 1), :, lanes_of(u)], arecv.at[d, s - 2, u])
-                if s < 4:
-                    gather_copy(d, s, u).start()
-            if s == 4:
-                gather_copy(outward, s, u).start()
+            for q in range(u * CHUNKS // 2, (u + 1) * CHUNKS // 2):
+                for d in range(2):
+                    landed(H.at[towards(1 - d, s - 1), chunk(q), :], arecv.at[d, s - 2, q])
+                    if s < 4:
+                        gather_copy(d, s, q).start()
+                if s == 4:
+                    gather_copy(outward, s, q).start()
+
+            def pair(d, _):
+                second_product((z + 8 + (2 * d - 1) * (s - 1)) % 8, u)
+                return 0
+
+            lax.fori_loop(0, 2, pair, 0)
+        if s == 2:
+            spread(2)
+            spread_on(0)
+            spread_on(1)
         if s == 3:
             landed(XO, xrecv.at[1, 1])
             cross_copy(3).start()
             cross_copy(4).start()
-
-        def pair(d, _):
-            second_product((z + 8 + (2 * d - 1) * (s - 1)) % 8)
-            return 0
-
-        lax.fori_loop(0, 2, pair, 0)
-        if s == 2:
-            spread(2)
-            spread_on(0)
-            spread_on(1)
         if s == 4:
             spread_on(2)
-            spread(3)
 
     for n in (5, 6, 7):
         loads[n].wait()
@@ -383,20 +407,20 @@
         jnp.broadcast_to(final_gain, (128, FB)).T[:, 0:1] * weights.astype(F32), axis=0, keepdims=True
     )
     for u in range(2):
-        landed(H.at[(z + 4) % 8, :, lanes_of(u)], arecv.at[inward, 3, u])
-    second_product((z + 4) % 8)
-
-    spread(4)
+        for q in range(u * CHUNKS // 2, (u + 1) * CHUNKS // 2):
+            landed(H.at[(z + 4) % 8, chunk(q), :], arecv.at[inward, 3, q])
+        second_product((z + 4) % 8, u)
+        spread(3 + u)
+
     landed(R, yrecv)
     spread_on(3)
-    mine = pl.ds(pl.multiple_of(w * SUB, SUB), SUB)
     row = lax.broadcasted_iota(jnp.int32, (8, 128), 0)
     columns = []
     for a in range(2):
         parts = []
         for b in range(4):
             t = 2 * b + a
-            u = E[t, mine, :] + out_bias + Yb[t, mine, :].astype(F32)
+            u = E[t, slot, :] + out_bias + Yb[t, slot, :].astype(F32)
             for k in range(7):
                 u = u + R[k, t].astype(F32)
             parts.append(u)
@@ -516,7 +540,7 @@
             pltpu.VMEM((QUARTER, FB), BF16),
             dma((10,)), dma, dma((4, 3)), dma, dma((4, 2)),
             dma, dma, dma, dma, dma((2,)), dma((2,)), dma((2,)), dma((2,)),
-            dma, dma((2, 4, 2)), dma, dma((2, 4, 2)),
+            dma, dma((2, 4, CHUNKS)), dma, dma((2, 4, CHUNKS)),
             dma, dma,
             dma((2, 2)), dma((2, 2)), dma((3,)), dma((3,)), dma((2,)), dma((2, 5)), dma,
         ],

time: 105 us -> 101 us (0.962)
  Pallas kernels: 103 us -> 99.4 us
    pallas_call x1, Pallas kernels: 101 us -> 97.1 us  [on_device(): pl.pallas_call(kernel, name='relayout_forward', out_shape=(jax.ShapeDtype...]
where the time goes in v6:
time: 101 us
  Pallas kernels  99.4 us (98%)
  between operations  1.45 us (1%)
    pallas_call x1, Pallas kernels, on_device(): pl.pallas_call(kernel, name='relayout_forward', out_shape=(jax.ShapeDtype...  97.1 us
    pallas_call x1, Pallas kernels, on_device(): pl.pallas_call(write_out, name='write_out', out_shape=(jax.ShapeDtypeStru...  2.23 us

profile of v6, /device:TPU:24, one launch (start us, length us, event | category | flops | bytes accessed | tf_op | source)
XLA Modules:
  0.0 100.8 jit_solution(14234086789069707534)
XLA Ops:
  1.3 97.1 %relayout_forward.1 = (bf16[2,768,768]{2,1,0:T(8,128)(2,1)S(1)}, bf16[768,1536]{1,0:T(8,128)(2,1)S(1)}, f32[64,128]{1,0:T(8,128)S(1)}) custom-call(bf16[4,16,588]{2,1,0:T(8,128)(2,1)} %bitcast.3, bf16[588,1536]{1,0:T(8,128)(2,1)} %embed_w.1, f32[1536]{0:T(1024)} %embed_b.1, bf16[1,768,1536]{2,1,0:T(8,128)(2,1)} %old_in.1, bf16[1,1536,768]{2,1,0:T(8,128)(2,1)} %old_out.1, ...), custom_call_target="tpu_custom_call" | custom-call | tf_op jit(solution)/shard_map/relayout_forward/pallas_call | solution.py:501
  98.4 2.2 %write_out.1 = (bf16[1536,768]{1,0:T(8,128)(2,1)}, bf16[768,1536]{1,0:T(8,128)(2,1)}, f32[64,128]{1,0:T(8,128)}) custom-call(bf16[1536,768]{1,0:T(8,128)(2,1)S(1)} %bitcast.2, bf16[768,1536]{1,0:T(8,128)(2,1)S(1)} %get-tuple-element.7.new_out, f32[64,128]{1,0:T(8,128)S(1)} %get-tuple-element.8.logits), custom_call_target="tpu_custom_call" | custom-call | tf_op jit(solution)/shard_map/write_out/pallas_call | solution.py:554

commit v7 on v6

--- a/solution.py
+++ b/solution.py
@@ -31,7 +31,7 @@
     P_, We, be, IT, OT, gt, ibt, obt, fg, Wc,
     E, st, stall, qown, qall, bsrc, bb, PP, rf, C, H, Yb, R, LB, LR, T, TR, XI, XO,
     lsem, psend, precv, dsend, drecv, ssend, srecv, qsend, qrecv, fsend, frecv, bsend, brecv,
-    rsend, rrecv, asend, arecv, ysend, yrecv, xsend, xrecv, zsend, zrecv, gsend, grecv, gend,
+    rsend, rrecv, asend, ysend, yrecv, xsend, xrecv, zsend, zrecv, gsend, grecv, gend,
 ):
     y, h, col = lax.axis_index("rep"), lax.axis_index("row"), lax.axis_index("col")
     l, w = col // 8, col % 8
@@ -67,8 +67,6 @@
     ]
     own = pltpu.make_async_copy(patches, P_.at[:, l, slot, :], lsem.at[9])
     own.start()
-    for load in loads:
-        load.start()
 
     barrier = pltpu.get_barrier_semaphore()
     peers = [at(y, 2 * h + (l + a) % 2, (w + b) % 8) for a in range(2) for b in range(8) if a or b]
@@ -78,6 +76,8 @@
     for peer in peers:
         pl.semaphore_signal(barrier, inc=1, device_id=peer, device_id_type=MESH)
     own.wait()
+    for load in loads:
+        load.start()
     pl.semaphore_wait(barrier, len(peers))
 
     partner = at(y, z, 2 * x + 1 - c)
@@ -108,35 +108,40 @@
         for k in range(4 if v == 0 else 1):
             partner_copy(v, k, c).start()
 
-    send_own(0)
-    for v in range(4):
-        patch_copy(v, 4).start()
-
-    loads[3].wait()
-    bsrc[...] = jnp.broadcast_to(ibt[pl.ds(rid[0], 1), :], bsrc.shape)
-    bias_to = 4 * l + x
-
-    def bias_copies(act):
-        for a in range(2):
-            is_self = jnp.logical_and(l == a, w == bias_to)
-
-            @pl.when(is_self)
-            def _():
-                if act == "start":
-                    pltpu.make_async_copy(bsrc, bb.at[c], brecv.at[c]).start()
-
-            @pl.when(jnp.logical_not(is_self))
-            def _():
-                copy = remote(bsrc, bb.at[c], bsend.at[a], brecv.at[c], at(y, 2 * h + a, bias_to))
-                copy.start() if act == "start" else copy.wait_send()
-
-    bias_copies("start")
-
     def pass_on(v):
         arrived(1, precv.at[v, 1])
         for k in range(5, 8):
             patch_copy(v, k).start()
         partner_copy(v, 4, c).start()
+
+    send_own(0)
+    for v in range(4):
+        patch_copy(v, 4).start()
+
+    pass_on(0)
+    pass_on(1)
+    send_own(1)
+    send_own(2)
+
+    loads[3].wait()
+    bsrc[...] = jnp.broadcast_to(ibt[pl.ds(rid[0], 1), :], bsrc.shape)
+    bias_to = 4 * l + x
+
+    def bias_copies(act):
+        for a in range(2):
+            is_self = jnp.logical_and(l == a, w == bias_to)
+
+            @pl.when(is_self)
+            def _():
+                if act == "start":
+                    pltpu.make_async_copy(bsrc, bb.at[c], brecv.at[c]).start()
+
+            @pl.when(jnp.logical_not(is_self))
+            def _():
+                copy = remote(bsrc, bb.at[c], bsend.at[a], brecv.at[c], at(y, 2 * h + a, bias_to))
+                copy.start() if act == "start" else copy.wait_send()
+
+    bias_copies("start")
 
     def share(v, plane):
         arrived(3, precv.at[v, 2 * plane])
@@ -219,10 +224,6 @@
 
         lax.fori_loop(0, 2, one, 0)
 
-    pass_on(0)
-    pass_on(1)
-    send_own(1)
-    send_own(2)
     share(0, 0)
     complete(0, 0)
     first_product(4)
@@ -345,7 +346,7 @@
 
     def gather_copy(d, s, q):
         ref = H.at[towards(1 - d, s - 1), chunk(q), :]
-        return remote(ref, ref, asend, arecv.at[d, s - 1, q], at(y, towards(d, 1), w))
+        return remote(ref, ref, asend, rrecv.at[d, s - 1, q], at(y, towards(d, 1), w))
 
     for q in range(CHUNKS):
         rows = slice(q * CHUNK, (q + 1) * CHUNK)
@@ -376,7 +377,7 @@
         for u in range(2):
             for q in range(u * CHUNKS // 2, (u + 1) * CHUNKS // 2):
                 for d in range(2):
-                    landed(H.at[towards(1 - d, s - 1), chunk(q), :], arecv.at[d, s - 2, q])
+                    landed(H.at[towards(1 - d, s - 1), chunk(q), :], rrecv.at[d, s - 2, q])
                     if s < 4:
                         gather_copy(d, s, q).start()
                 if s == 4:
@@ -395,7 +396,6 @@
             landed(XO, xrecv.at[1, 1])
             cross_copy(3).start()
             cross_copy(4).start()
-        if s == 4:
             spread_on(2)
 
     for n in (5, 6, 7):
@@ -408,7 +408,7 @@
     )
     for u in range(2):
         for q in range(u * CHUNKS // 2, (u + 1) * CHUNKS // 2):
-            landed(H.at[(z + 4) % 8, chunk(q), :], arecv.at[inward, 3, q])
+            landed(H.at[(z + 4) % 8, chunk(q), :], rrecv.at[inward, 3, q])
         second_product((z + 4) % 8, u)
         spread(3 + u)
 
@@ -540,7 +540,7 @@
             pltpu.VMEM((QUARTER, FB), BF16),
             dma((10,)), dma, dma((4, 3)), dma, dma((4, 2)),
             dma, dma, dma, dma, dma((2,)), dma((2,)), dma((2,)), dma((2,)),
-            dma, dma((2, 4, CHUNKS)), dma, dma((2, 4, CHUNKS)),
+            dma, dma((2, 4, CHUNKS)), dma,
             dma, dma,
             dma((2, 2)), dma((2, 2)), dma((3,)), dma((3,)), dma((2,)), dma((2, 5)), dma,
         ],

time: 101 us -> 100 us (0.990)
  Pallas kernels: 99.4 us -> 98.2 us
    pallas_call x1, Pallas kernels: 97.1 us -> 95.9 us  [on_device(): pl.pallas_call(kernel, name='relayout_forward', out_shape=(jax.ShapeDtype...]
where the time goes in v7:
time: 100 us; the launch traced here: 99.6 us
  Pallas kernels  98.2 us (98%)
  between operations  1.45 us (1%)
    pallas_call x1, Pallas kernels, on_device(): pl.pallas_call(kernel, name='relayout_forward', out_shape=(jax.ShapeDtype...  95.9 us
    pallas_call x1, Pallas kernels, on_device(): pl.pallas_call(write_out, name='write_out', out_shape=(jax.ShapeDtypeStru...  2.23 us

profile of v7, /device:TPU:24, one launch (start us, length us, event | category | flops | bytes accessed | tf_op | source)
XLA Modules:
  0.0 99.6 jit_solution(3421740969154442577)
XLA Ops:
  1.3 95.9 %relayout_forward.1 = (bf16[2,768,768]{2,1,0:T(8,128)(2,1)S(1)}, bf16[768,1536]{1,0:T(8,128)(2,1)S(1)}, f32[64,128]{1,0:T(8,128)S(1)}) custom-call(bf16[4,16,588]{2,1,0:T(8,128)(2,1)} %bitcast.3, bf16[588,1536]{1,0:T(8,128)(2,1)} %embed_w.1, f32[1536]{0:T(1024)} %embed_b.1, bf16[1,768,1536]{2,1,0:T(8,128)(2,1)} %old_in.1, bf16[1,1536,768]{2,1,0:T(8,128)(2,1)} %old_out.1, ...), custom_call_target="tpu_custom_call" | custom-call | tf_op jit(solution)/shard_map/relayout_forward/pallas_call | solution.py:501
  97.2 2.2 %write_out.1 = (bf16[1536,768]{1,0:T(8,128)(2,1)}, bf16[768,1536]{1,0:T(8,128)(2,1)}, f32[64,128]{1,0:T(8,128)}) custom-call(bf16[1536,768]{1,0:T(8,128)(2,1)S(1)} %bitcast.2, bf16[768,1536]{1,0:T(8,128)(2,1)S(1)} %get-tuple-element.7.new_out, f32[64,128]{1,0:T(8,128)S(1)} %get-tuple-element.8.logits), custom_call_target="tpu_custom_call" | custom-call | tf_op jit(solution)/shard_map/write_out/pallas_call | solution.py:554

commit v8 on v7

--- a/solution.py
+++ b/solution.py
@@ -263,9 +263,9 @@
                         copy.start() if act == "start" else copy.wait_send()
 
     share(0, 1)
+    share(1, 1)
     complete(0, 1)
     first_product(5 - 2 * l)
-    share(1, 1)
     complete(1, 1)
     first_product(3 + 2 * l)
     share(1, 0)

time: 100 us -> 99.4 us (level)
  no operation moved by 1% of the time
where the time goes in v8:
time: 99.4 us; the launch traced here: 98.9 us
  Pallas kernels  97.5 us (98%)
  between operations  1.45 us (1%)
    pallas_call x1, Pallas kernels, on_device(): pl.pallas_call(kernel, name='relayout_forward', out_shape=(jax.ShapeDtype...  95.3 us
    pallas_call x1, Pallas kernels, on_device(): pl.pallas_call(write_out, name='write_out', out_shape=(jax.ShapeDtypeStru...  2.23 us

profile of v8, /device:TPU:24, one launch (start us, length us, event | category | flops | bytes accessed | tf_op | source)
XLA Modules:
  0.0 98.9 jit_solution(13338507610137766283)
XLA Ops:
  1.3 95.3 %relayout_forward.1 = (bf16[2,768,768]{2,1,0:T(8,128)(2,1)S(1)}, bf16[768,1536]{1,0:T(8,128)(2,1)S(1)}, f32[64,128]{1,0:T(8,128)S(1)}) custom-call(bf16[4,16,588]{2,1,0:T(8,128)(2,1)} %bitcast.3, bf16[588,1536]{1,0:T(8,128)(2,1)} %embed_w.1, f32[1536]{0:T(1024)} %embed_b.1, bf16[1,768,1536]{2,1,0:T(8,128)(2,1)} %old_in.1, bf16[1,1536,768]{2,1,0:T(8,128)(2,1)} %old_out.1, ...), custom_call_target="tpu_custom_call" | custom-call | tf_op jit(solution)/shard_map/relayout_forward/pallas_call | solution.py:501
  96.6 2.2 %write_out.1 = (bf16[1536,768]{1,0:T(8,128)(2,1)}, bf16[768,1536]{1,0:T(8,128)(2,1)}, f32[64,128]{1,0:T(8,128)}) custom-call(bf16[1536,768]{1,0:T(8,128)(2,1)S(1)} %bitcast.2, bf16[768,1536]{1,0:T(8,128)(2,1)S(1)} %get-tuple-element.7.new_out, f32[64,128]{1,0:T(8,128)S(1)} %get-tuple-element.8.logits), custom_call_target="tpu_custom_call" | custom-call | tf_op jit(solution)/shard_map/write_out/pallas_call | solution.py:554

commit v9 on v8

--- a/solution.py
+++ b/solution.py
@@ -161,18 +161,6 @@
         return jnp.where(l == 0, v[:, :FB], v[:, FB:])
 
     embed_bias = my_half(be)
-    gains16 = jnp.broadcast_to(gain, (16, FB))
-    gains_hi = gains16.astype(BF16)
-    gains_lo = (gains16 - gains_hi.astype(F32)).astype(BF16)
-    product = jnp.dot(gains_hi, IT[...], preferred_element_type=F32)
-    product = product + jnp.dot(gains_lo, IT[...], preferred_element_type=F32)
-    qown[...] = product[0:1, :]
-
-    def q_copy(k):
-        return remote(qown, qall.at[k], qsend, qrecv, at(y, (z + k) % 8, w))
-
-    for k in range(1, 8):
-        q_copy(k).start()
     lane = lax.broadcasted_iota(jnp.int32, (TB, 128), 1)
 
     def stat_copy(k):
@@ -262,6 +250,18 @@
                         copy = remote(src, dst, xsend.at[a, u], xrecv.at[a, n], dev)
                         copy.start() if act == "start" else copy.wait_send()
 
+    gains16 = jnp.broadcast_to(gain, (16, FB))
+    gains_hi = gains16.astype(BF16)
+    gains_lo = (gains16 - gains_hi.astype(F32)).astype(BF16)
+    product = jnp.dot(gains_hi, IT[...], preferred_element_type=F32)
+    product = product + jnp.dot(gains_lo, IT[...], preferred_element_type=F32)
+    qown[...] = product[0:1, :]
+
+    def q_copy(k):
+        return remote(qown, qall.at[k], qsend, qrecv, at(y, (z + k) % 8, w))
+
+    for k in range(1, 8):
+        q_copy(k).start()
     share(0, 1)
     share(1, 1)
     complete(0, 1)

time: 99.4 us -> 101 us (1.016)
  no operation moved by 1% of the time
where the time goes in v9:
time: 101 us; the launch traced here: 99.7 us
  Pallas kernels  98.2 us (97%)
  between operations  1.45 us (1%)
    pallas_call x1, Pallas kernels, on_device(): pl.pallas_call(kernel, name='relayout_forward', out_shape=(jax.ShapeDtype...  96 us
    pallas_call x1, Pallas kernels, on_device(): pl.pallas_call(write_out, name='write_out', out_shape=(jax.ShapeDtypeStru...  2.23 us

profile of v9, /device:TPU:24, one launch (start us, length us, event | category | flops | bytes accessed | tf_op | source)
XLA Modules:
  0.0 99.7 jit_solution(15817034657049893775)
XLA Ops:
  1.3 96.0 %relayout_forward.1 = (bf16[2,768,768]{2,1,0:T(8,128)(2,1)S(1)}, bf16[768,1536]{1,0:T(8,128)(2,1)S(1)}, f32[64,128]{1,0:T(8,128)S(1)}) custom-call(bf16[4,16,588]{2,1,0:T(8,128)(2,1)} %bitcast.3, bf16[588,1536]{1,0:T(8,128)(2,1)} %embed_w.1, f32[1536]{0:T(1024)} %embed_b.1, bf16[1,768,1536]{2,1,0:T(8,128)(2,1)} %old_in.1, bf16[1,1536,768]{2,1,0:T(8,128)(2,1)} %old_out.1, ...), custom_call_target="tpu_custom_call" | custom-call | tf_op jit(solution)/shard_map/relayout_forward/pallas_call | solution.py:501
  97.3 2.2 %write_out.1 = (bf16[1536,768]{1,0:T(8,128)(2,1)}, bf16[768,1536]{1,0:T(8,128)(2,1)}, f32[64,128]{1,0:T(8,128)}) custom-call(bf16[1536,768]{1,0:T(8,128)(2,1)S(1)} %bitcast.2, bf16[768,1536]{1,0:T(8,128)(2,1)S(1)} %get-tuple-element.7.new_out, f32[64,128]{1,0:T(8,128)S(1)} %get-tuple-element.8.logits), custom_call_target="tpu_custom_call" | custom-call | tf_op jit(solution)/shard_map/write_out/pallas_call | solution.py:554
